TPU v7x, 32 devices: a whole 2x2x4 slice. The times are simulated.
32 devices in a mesh: user: 16 (over z, y, x), seq: 2 (over core).
Axes of the slice: x: 2, y: 2, z: 4, core: 2. Of those that a mesh axis runs over, the one named last changes fastest.
Arguments:
- behaviors: bfloat16 [32, 2048, 256], P('user', 'seq'), may hold values from -20 to 20
- candidates: bfloat16 [32, 64, 256], P('user', 'seq'), may hold values from -64 to 64
- ranks: int32 [32, 2, 128], P('user', 'seq'), may hold values from 0 to 1151, as said below
- lengths: int32 [32], P('user'), may hold values from 1024 to 2048
- hash_planes: bfloat16 [256, 64], replicated, may hold values from -0.375 to 0.375
- norm_gain: float32 [256], replicated, may hold values from 0.5 to 1.5
- norm_bias: float32 [256], replicated, may hold values from -3 to 3
Outputs:
- interest: bfloat16 [32, 64, 256], P('user', 'seq')
Inputs may be any that keep to these rules, and one draw needn't show every extreme that they name: ranks[u, s, :] are 128 distinct positions of group s's window of 1152 behaviors; on the first group all are 128 or more.
All inputs are finite; a program needn't handle non-finite values.
Results may differ from a plain program's by a relative error of at most 0.0023.
Values may be sent and summed in bfloat16 or wider, within the bound.
No kernel may reach another device: no remote copies, remote signals or barrier semaphores. Data moves between devices by JAX's collectives and lax.ppermute only.
A program may use at most 64 MiB of HBM per device.

v0:
```python
import math

import jax
import jax.numpy as jnp
from jax import lax
from jax.sharding import PartitionSpec as P

HALO = 128


NEG_FILL = -1e30
HASH_WEIGHT = 2.0
NORM_EPS = 1e-05


def passed_along(value, axis, steps):
    count = lax.axis_size(axis)
    first, last = (max(0, -steps), min(count, count - steps))
    return lax.ppermute(value, axis, [(source, source + steps) for source in range(first, last)])


def joined(shard, axis, combine):
    everything = jax.tree.map(lambda part: lax.all_gather(part, axis), shard)
    first = jax.tree.map(lambda part: part[0], everything)

    def turn(k, so_far):
        return combine(so_far, jax.tree.map(lambda part: part[k], everything))

    return lax.fori_loop(1, lax.axis_size(axis), turn, first)


def soft_codes(rows, hash_planes):
    return jnp.tanh(jnp.dot(rows, hash_planes, preferred_element_type=jnp.float32)).astype(
        jnp.bfloat16
    )


def combine_parts(left_part, right_part):
    joint_max = jnp.maximum(left_part[0], right_part[0])
    left_scale = jnp.exp(left_part[0] - joint_max)
    right_scale = jnp.exp(right_part[0] - joint_max)
    total_sum = left_part[1] * left_scale + right_part[1] * right_scale
    vector_sum = left_part[2] * left_scale[..., None] + right_part[2] * right_scale[..., None]
    return (joint_max, total_sum, vector_sum)


def shards(behaviors, candidates, ranks, lengths, hash_planes, norm_gain, norm_bias):
    group_rows = behaviors.shape[1]
    feature_width = behaviors.shape[2]
    own_cands = candidates.shape[1]
    code_bits = hash_planes.shape[1]
    seq_index = lax.axis_index("seq")
    tail_rows = behaviors[:, group_rows - HALO :, :]
    before = passed_along(tail_rows, "seq", 1)
    queries = lax.all_gather(candidates, "seq", axis=1, tiled=True)
    window_pos = ranks[:, 0, :]
    from_tail = window_pos < HALO
    tail_index = jnp.clip(window_pos, 0, HALO - 1)
    own_index = jnp.clip(window_pos - HALO, 0, group_rows - 1)
    take_rows = jax.vmap(lambda row_table, where_at: row_table[where_at])
    picked = jnp.where(
        from_tail[:, :, None], take_rows(before, tail_index), take_rows(behaviors, own_index)
    )
    position = seq_index * group_rows - HALO + window_pos
    usable = (position >= 0) & (position < lengths[:, None])
    query_codes = soft_codes(queries, hash_planes)
    picked_codes = soft_codes(picked, hash_planes)
    similar = jnp.einsum("ucd,ukd->uck", queries, picked, preferred_element_type=jnp.float32)
    agreement = jnp.einsum(
        "ucb,ukb->uck", query_codes, picked_codes, preferred_element_type=jnp.float32
    )
    scores = similar * (1.0 / math.sqrt(feature_width)) + HASH_WEIGHT / code_bits * agreement
    usable_rows = usable[:, None, :]
    group_max = jnp.max(jnp.where(usable_rows, scores, NEG_FILL), axis=2)
    weights = jnp.where(usable_rows, jnp.exp(scores - group_max[..., None]), 0.0)
    group_total = jnp.sum(weights, axis=2)
    group_sum = jnp.einsum(
        "uck,ukd->ucd", weights.astype(jnp.bfloat16), picked, preferred_element_type=jnp.float32
    )
    merged = joined((group_max, group_total, group_sum), "seq", combine_parts)
    denominator = lax.dynamic_slice_in_dim(merged[1], seq_index * own_cands, own_cands, 1)
    numerator = lax.dynamic_slice_in_dim(merged[2], seq_index * own_cands, own_cands, 1)
    attended = numerator / denominator[..., None]
    moments = lax.psum(
        (jnp.sum(attended, axis=(0, 1)), jnp.sum(attended * attended, axis=(0, 1))), ("user", "seq")
    )
    row_count = attended.shape[0] * own_cands * lax.axis_size("user") * lax.axis_size("seq")
    feature_mean = moments[0] / row_count
    feature_var = moments[1] / row_count - feature_mean * feature_mean
    normed = (attended - feature_mean) * lax.rsqrt(feature_var + NORM_EPS) * norm_gain + norm_bias
    return normed.astype(jnp.bfloat16)


def solution(mesh):
    in_specs = (
        P("user", "seq", None),
        P("user", "seq", None),
        P("user", "seq", None),
        P("user"),
        P(),
        P(),
        P(),
    )
    out_specs = P("user", "seq", None)
    return jax.shard_map(shards, mesh=mesh, in_specs=in_specs, out_specs=out_specs, check_vma=False)
```

profile of v0, /device:TPU:0, one launch (start us, length us, event | category | flops | bytes accessed | tf_op | source)
XLA Modules:
  0.0 59.7 jit_solution(5533782162240582082)
XLA Ops:
  0.0 0.0 copy-start
  0.0 0.0 copy-start.2
  0.0 0.0 copy-start.5
  0.0 0.9 %slice.15 = bf16[2,128,256]{2,1,0:T(8,128)(2,1)S(1)} slice(bf16[2,1024,256]{2,1,0:T(8,128)(2,1)} %param.7), slice={[0:2], [896:1024], [0:256]} | slice | bytes 262144 | tf_op jit(solution)/shard_map/slice | solution.py:53
  1.0 0.0 copy-start.1
  1.0 2.4 %collective-permute-start = (bf16[2,128,256]{2,1,0:T(8,128)(2,1)S(1)}, bf16[2,128,256]{2,1,0:T(8,128)(2,1)S(1)}, u32[]{:S(2)}, u32[]{:S(2)}) collective-permute-start(bf16[2,128,256]{2,1,0:T(8,128)(2,1)S(1)} %slice.15), channel_id=1, source_target_pairs={{0,1},{2,3},{4,5},{6,7},{8,9},{10,11},{12,13},{14,15},{16,17},{18,... | collective-permute-start | bytes 393224 | tf_op jit(solution)/shard_map/ppermute | solution.py:19
  3.4 0.0 copy-done.2
  3.4 0.0 copy-done.5
  3.4 0.1 compare_and_fusion
  3.5 0.0 copy-done.1
  3.5 1.9 %all_gather.21 = bf16[2,64,256]{2,1,0:T(8,128)(2,1)S(1)} all-gather(bf16[2,32,256]{2,1,0:T(8,128)(2,1)S(1)} %copy-done.1), channel_id=1, replica_groups=mesh['user'=16,'seq'=2] {'seq'}, dimensions={1}, use_global_device_ids=true | all-gather | bytes 98304 | tf_op jit(solution)/shard_map/all_gather | solution.py:55
  5.4 2.8 %gather_fusion.1 = bf16[256,256]{1,0:T(8,128)(2,1)S(1)} fusion(bf16[2,1024,256]{2,1,0:T(8,128)(2,1)} %param.7, s32[256]{0:T(256)S(1)} %fusion.27), kind=kCustom, calls=%fused_computation.1 | custom fusion | bytes 264192 | tf_op jit(solution)/shard_map/vmap()/gather | solution.py:60
  8.2 0.0 copy-done
  8.2 0.1 fusion.2
  8.3 0.0 collective-permute-done
  8.4 1.7 %gather_fusion = bf16[256,256]{1,0:T(8,128)(2,1)S(1)} fusion(bf16[2,128,256]{2,1,0:T(8,128)(2,1)S(1)} %collective-permute-done, s32[256]{0:T(256)S(1)} %fusion.28), kind=kCustom, calls=%fused_computation | custom fusion | bytes 264192 | tf_op jit(solution)/shard_map/vmap()/gather | solution.py:60
  10.0 0.1 broadcast_select_fusion
  10.1 0.2 fusion.1
  10.3 0.4 select_reduce_fusion
  10.7 0.2 fusion.8
  10.9 0.2 fusion.6
  11.1 1.8 %all-gather.3 = f32[2,2,64]{2,1,0:T(2,128)S(1)} all-gather(f32[1,2,64]{2,1,0:T(2,128)S(1)} %bitcast.67), channel_id=3, replica_groups=mesh['user'=16,'seq'=2] {'seq'}, dimensions={0}, use_global_device_ids=true | all-gather | bytes 1536 | tf_op jit(solution)/shard_map/all_gather | solution.py:23
  12.9 1.8 %all-gather.4 = f32[2,2,64]{2,1,0:T(2,128)S(1)} all-gather(f32[1,2,64]{2,1,0:T(2,128)S(1)} %bitcast.72), channel_id=4, replica_groups=mesh['user'=16,'seq'=2] {'seq'}, dimensions={0}, use_global_device_ids=true | all-gather | bytes 1536 | tf_op jit(solution)/shard_map/all_gather | solution.py:23
  14.7 2.0 %all-gather = f32[4,64,256]{2,1,0:T(8,128)S(1)} all-gather(f32[2,64,256]{2,1,0:T(8,128)S(1)} %fusion.8), channel_id=2, replica_groups=mesh['user'=16,'seq'=2] {'seq'}, dimensions={0}, use_global_device_ids=true | all-gather | bytes 393216 | tf_op jit(solution)/shard_map/all_gather | solution.py:23
  16.7 0.1 constant_dynamic-slice_fusion.2
  16.8 0.1 constant_dynamic-slice_fusion
  16.9 0.0 copy-start.4
  16.9 0.1 fusion.30
  17.0 41.3 %all-reduce = (f32[256]{0:T(256)S(1)}, f32[256]{0:T(256)S(1)}) all-reduce(f32[256]{0:T(256)S(1)} %get-tuple-element.20, f32[256]{0:T(256)S(1)} %get-tuple-element.19), channel_id=1, replica_groups=mesh['user'=16,'seq'=2] {'user','seq'}, use_global_device_ids=true, to_apply=%region_5.6 | all-reduce | flops 512 | bytes 4096 | tf_op jit(solution)/shard_map/psum | solution.py:84
  58.4 0.0 copy-start.3
  58.4 0.0 copy-done.4
  58.4 0.7 %copy-done.3 = f32[256]{0:T(256)S(1)} copy-done((f32[256]{0:T(256)S(1)}, f32[256]{0:T(256)}, u32[]{:S(2)}) %copy-start.3) | copy-done | bytes 1048
  59.0 0.6 %add_convert_fusion = bf16[2,32,256]{2,1,0:T(8,128)(2,1)} fusion(f32[2,32,256]{2,1,0:T(8,128)S(1)} %get-tuple-element.23, f32[256]{0:T(256)S(1)} %copy-done.3, f32[256]{0:T(256)S(1)} %copy-done.4, f32[256]{0:T(256)S(1)} %get-tuple-element.40, f32[256]{0:T(256)S(1)} %get-tuple-element.39), kind=kLoop, calls=%fused_computation.15 | loop fusion | flops 81920 | bytes 102400 | tf_op jit(solution)/shard_map/convert_element_type | solution.py:91
  (9 shorter events, 0.1 us)
Async XLA Ops:
  0.0 8.2 %copy-start = (bf16[256,64]{0,1:T(8,128)(2,1)S(1)}, bf16[256,64]{0,1:T(8,128)(2,1)}, u32[]{:S(2)}) copy-start(bf16[256,64]{0,1:T(8,128)(2,1)} %param.11) | copy-start | bytes 98308
  0.0 3.4 %copy-start.2 = (s32[2,1,128]{2,1,0:T(1,128)S(1)}, s32[2,1,128]{2,1,0:T(1,128)}, u32[]{:S(2)}) copy-start(s32[2,1,128]{2,1,0:T(1,128)} %param.9) | copy-start | bytes 3076
  0.0 3.4 %copy-start.5 = (s32[2]{0:T(128)S(1)}, s32[2]{0:T(128)}, u32[]{:S(2)}) copy-start(s32[2]{0:T(128)} %param.10) | copy-start | bytes 28
  1.0 2.6 %copy-start.1 = (bf16[2,32,256]{2,1,0:T(8,128)(2,1)S(1)}, bf16[2,32,256]{2,1,0:T(8,128)(2,1)}, u32[]{:S(2)}) copy-start(bf16[2,32,256]{2,1,0:T(8,128)(2,1)} %param.8) | copy-start | bytes 98308
  1.0 7.4 %collective-permute-start = (bf16[2,128,256]{2,1,0:T(8,128)(2,1)S(1)}, bf16[2,128,256]{2,1,0:T(8,128)(2,1)S(1)}, u32[]{:S(2)}, u32[]{:S(2)}) collective-permute-start(bf16[2,128,256]{2,1,0:T(8,128)(2,1)S(1)} %slice.15), channel_id=1, source_target_pairs={{0,1},{2,3},{4,5},{6,7},{8,9},{10,11},{12,13},{14,15},{16,17},{18,... | collective-permute-start | bytes 393224 | tf_op jit(solution)/shard_map/ppermute | solution.py:19
  16.9 41.5 %copy-start.4 = (f32[256]{0:T(256)S(1)}, f32[256]{0:T(256)}, u32[]{:S(2)}) copy-start(f32[256]{0:T(256)} %param.12) | copy-start | bytes 3076
  58.4 0.7 %copy-start.3 = (f32[256]{0:T(256)S(1)}, f32[256]{0:T(256)}, u32[]{:S(2)}) copy-start(f32[256]{0:T(256)} %param.13) | copy-start | bytes 3076
where the time goes:
time: 60 us; the launch traced here: 59.7 us
  blocking collectives  48.8 us (81%)
  local copies, waits for them, and re-layouts  6.23 us (10%)
  starting transfers between devices  2.41 us (4%)
  other arithmetic  1.14 us (2%)
  matrix products  0.95 us (2%)
    psum x1, blocking collectives, shards(): lax.psum((jnp.sum(attended, axis=(0, 1)), jnp.sum(attended * attended, ax...  41.3 us
    all_gather x3, blocking collectives, joined(): everything = jax.tree.map(lambda part: lax.all_gather(part, axis), shard)  5.58 us
    gather x2, local copies, waits for them, and re-layouts, shards(): take_rows = jax.vmap(lambda row_table, where_at: row_table[where_at])  4.41 us
    ppermute x1, starting transfers between devices, passed_along(): lax.ppermute(value, axis, [(source, source + steps) for source in range(f...  2.41 us
    all_gather x1, blocking collectives, shards(): queries = lax.all_gather(candidates, 'seq', axis=1, tiled=True)  1.85 us
  transfers between devices with their start and end apart: 1, of which 0 were waited for; matrix products, arithmetic and copies ran while one was open for 5% of the time, Pallas kernels for 0%

commit v1 on v0

v1 whole, which is shorter than its diff:
```python
import math

import jax
import jax.numpy as jnp
from jax import lax
from jax.sharding import PartitionSpec as P

HALO = 128


NEG_FILL = -1e30
HASH_WEIGHT = 2.0
NORM_EPS = 1e-05

BOTH = ("user", "seq")


def swapped_index(seq_index, seq_count):
    return seq_index ^ 1 if seq_count % 2 == 0 else seq_index


def user_total(value):
    users, seqs = lax.axis_size("user"), lax.axis_size("seq")
    if users & (users - 1):
        return lax.psum(value, "user")
    stride = 1
    while stride < users:
        pairs = [
            (user * seqs + seq, (user ^ stride) * seqs + swapped_index(seq, seqs))
            for user in range(users)
            for seq in range(seqs)
        ]
        value = value + lax.ppermute(value, BOTH, pairs)
        stride *= 2
    return value


def seq_parts(value):
    seqs = lax.axis_size("seq")
    if seqs == 2:
        return [value, lax.ppermute(value, "seq", [(0, 1), (1, 0)])]
    everything = lax.all_gather(value, "seq")
    return [everything[k] for k in range(seqs)]


def soft_codes(rows, hash_planes):
    return jnp.tanh(jnp.dot(rows, hash_planes, preferred_element_type=jnp.float32)).astype(
        jnp.bfloat16
    )


def shards(behaviors, candidates, ranks, lengths, hash_planes, norm_gain, norm_bias):
    group_rows = behaviors.shape[1]
    feature_width = behaviors.shape[2]
    own_cands = candidates.shape[1]
    code_bits = hash_planes.shape[1]
    seqs = lax.axis_size("seq")
    seq_index = lax.axis_index("seq")
    tail_rows = behaviors[:, group_rows - HALO :, :]
    before = lax.ppermute(tail_rows, "seq", [(k, (k + 1) % seqs) for k in range(seqs)])
    queries = lax.all_gather(candidates, "seq", axis=1, tiled=True)
    window_pos = ranks[:, 0, :]
    from_tail = window_pos < HALO
    tail_index = jnp.clip(window_pos, 0, HALO - 1)
    own_index = jnp.clip(window_pos - HALO, 0, group_rows - 1)
    take_rows = jax.vmap(lambda row_table, where_at: row_table[where_at])
    picked = jnp.where(
        from_tail[:, :, None], take_rows(before, tail_index), take_rows(behaviors, own_index)
    )
    position = seq_index * group_rows - HALO + window_pos
    usable = (position >= 0) & (position < lengths[:, None])
    query_codes = soft_codes(queries, hash_planes)
    picked_codes = soft_codes(picked, hash_planes)
    similar = jnp.einsum("ucd,ukd->uck", queries, picked, preferred_element_type=jnp.float32)
    agreement = jnp.einsum(
        "ucb,ukb->uck", query_codes, picked_codes, preferred_element_type=jnp.float32
    )
    scores = similar * (1.0 / math.sqrt(feature_width)) + HASH_WEIGHT / code_bits * agreement
    usable_rows = usable[:, None, :]
    group_max = jnp.max(jnp.where(usable_rows, scores, NEG_FILL), axis=2)
    weights = jnp.where(usable_rows, jnp.exp(scores - group_max[..., None]), 0.0)
    group_total = jnp.sum(weights, axis=2)
    group_sum = jnp.einsum(
        "uck,ukd->ucd", weights.astype(jnp.bfloat16), picked, preferred_element_type=jnp.float32
    )
    cands = group_sum.shape[1]
    side = jnp.broadcast_to(
        jnp.stack([group_max, group_total], axis=2)[..., None], group_sum.shape[:2] + (2, 64)
    ).reshape(group_sum.shape[:2] + (128,))
    parts = seq_parts(jnp.concatenate([group_sum, side], axis=2))
    tops = [part[:, :, feature_width] for part in parts]
    joint_max = tops[0]
    for top in tops[1:]:
        joint_max = jnp.maximum(joint_max, top)
    numerator, denominator = 0.0, 0.0
    for part, top in zip(parts, tops):
        rescale = jnp.exp(top - joint_max)
        numerator = numerator + rescale[..., None] * part[:, :, :feature_width]
        denominator = denominator + rescale * part[:, :, feature_width + 64]
    attended = numerator / denominator[..., None]
    moments = user_total(
        jnp.stack([jnp.sum(attended, axis=(0, 1)), jnp.sum(attended * attended, axis=(0, 1))])
    )
    row_count = attended.shape[0] * cands * lax.axis_size("user")
    feature_mean = moments[0] / row_count
    feature_var = moments[1] / row_count - feature_mean * feature_mean
    own = lax.dynamic_slice_in_dim(attended, seq_index * own_cands, own_cands, 1)
    normed = (own - feature_mean) * lax.rsqrt(feature_var + NORM_EPS) * norm_gain + norm_bias
    return normed.astype(jnp.bfloat16)


def solution(mesh):
    in_specs = (
        P("user", "seq", None),
        P("user", "seq", None),
        P("user", "seq", None),
        P("user"),
        P(),
        P(),
        P(),
    )
    out_specs = P("user", "seq", None)
    return jax.shard_map(shards, mesh=mesh, in_specs=in_specs, out_specs=out_specs, check_vma=False)
```

time: 60 us -> 28.8 us (0.48)
  blocking collectives: 48.8 us -> 1.85 us
  starting transfers between devices: 2.41 us -> 9.86 us
  waiting for transfers between devices: 0.01 us -> 6.51 us
  local copies, waits for them, and re-layouts: 6.23 us -> 7.8 us
    psum x1 -> x0, blocking collectives: 41.3 us -> none  [shards(): lax.psum((jnp.sum(attended, axis=(0, 1)), jnp.sum(attended * attended, ax...]
    ppermute x1 -> x6, starting transfers between devices: 2.41 us -> 9.86 us  [the longest x4 8.99 us: user_total(): value = value + lax.ppermute(value, BOTH, pairs)]
    ppermute x1 -> x6, waiting for transfers between devices: 0.01 us -> 6.51 us  [the longest x4 5.31 us: user_total(): value = value + lax.ppermute(value, BOTH, pairs)]
    all_gather x3 -> x0, blocking collectives: 5.58 us -> none  [joined(): everything = jax.tree.map(lambda part: lax.all_gather(part, axis), shard)]
    unnamed x14, local copies, waits for them, and re-layouts: 0.71 us -> 2.02 us
  transfers between devices with their start and end apart: 1 -> 6, of which waited for: 0 -> 5; matrix products, arithmetic and copies ran while one was open for 5% -> 11% of each run, Pallas kernels for 0% -> 0%
where the time goes in v1:
time: 28.8 us; the launch traced here: 28.5 us
  starting transfers between devices  9.86 us (34%)
  local copies, waits for them, and re-layouts  7.8 us (27%)
  waiting for transfers between devices  6.51 us (23%)
  blocking collectives  1.85 us (6%)
  other arithmetic  1.41 us (5%)
  matrix products  0.96 us (3%)
    ppermute x4, starting transfers between devices, user_total(): value = value + lax.ppermute(value, BOTH, pairs)  8.99 us
    ppermute x4, waiting for transfers between devices, user_total(): value = value + lax.ppermute(value, BOTH, pairs)  5.31 us
    gather x2, local copies, waits for them, and re-layouts, shards(): take_rows = jax.vmap(lambda row_table, where_at: row_table[where_at])  4.41 us
    unnamed x14, local copies, waits for them, and re-layouts  2.02 us
    all_gather x1, blocking collectives, shards(): queries = lax.all_gather(candidates, 'seq', axis=1, tiled=True)  1.85 us
    ppermute x1, waiting for transfers between devices, seq_parts(): return [value, lax.ppermute(value, 'seq', [(0, 1), (1, 0)])]  1.19 us
    slice x1, local copies, waits for them, and re-layouts, shards(): tail_rows = behaviors[:, group_rows - HALO:, :]  0.93 us
    convert_element_type x1, other arithmetic, shards(): return normed.astype(jnp.bfloat16)  0.63 us
  transfers between devices with their start and end apart: 6, of which 5 were waited for; matrix products, arithmetic and copies ran while one was open for 11% of the time, Pallas kernels for 0%

profile of v1, /device:TPU:0, one launch (start us, length us, event | category | flops | bytes accessed | tf_op | source)
XLA Modules:
  0.0 28.5 jit_solution(7570414600091922486)
XLA Ops:
  0.0 0.0 copy-start
  0.0 0.0 copy-start.1
  0.0 0.9 %slice.24 = bf16[2,128,256]{2,1,0:T(8,128)(2,1)S(1)} slice(bf16[2,1024,256]{2,1,0:T(8,128)(2,1)} %param.7), slice={[0:2], [896:1024], [0:256]} | slice | bytes 262144 | tf_op jit(solution)/shard_map/slice | solution.py:59
  0.9 0.6 %collective-permute-start = (bf16[2,128,256]{2,1,0:T(8,128)(2,1)S(1)}, bf16[2,128,256]{2,1,0:T(8,128)(2,1)S(1)}, u32[]{:S(2)}, u32[]{:S(2)}) collective-permute-start(bf16[2,128,256]{2,1,0:T(8,128)(2,1)S(1)} %slice.24), channel_id=1, source_target_pairs={{0,1},{1,0},{2,3},{3,2},{4,5},{5,4},{6,7},{7,6},{8,9},{9,8},{10,11... | collective-permute-start | bytes 393224 | tf_op jit(solution)/shard_map/ppermute | solution.py:60
  1.5 0.0 copy-start.2
  1.5 0.7 %copy-done.2 = s32[2,1,128]{2,1,0:T(1,128)S(1)} copy-done((s32[2,1,128]{2,1,0:T(1,128)S(1)}, s32[2,1,128]{2,1,0:T(1,128)}, u32[]{:S(2)}) %copy-start.2) | copy-done | bytes 1048
  2.2 0.0 copy-start.5
  2.2 0.6 %copy-done.5 = s32[2]{0:T(128)S(1)} copy-done((s32[2]{0:T(128)S(1)}, s32[2]{0:T(128)}, u32[]{:S(2)}) %copy-start.5) | copy-done | bytes 32
  2.9 0.1 compare_and_fusion
  2.9 0.0 copy-done.1
  3.0 1.9 %all_gather.3 = bf16[2,64,256]{2,1,0:T(8,128)(2,1)S(1)} all-gather(bf16[2,32,256]{2,1,0:T(8,128)(2,1)S(1)} %copy-done.1), channel_id=1, replica_groups=mesh['user'=16,'seq'=2] {'seq'}, dimensions={1}, use_global_device_ids=true | all-gather | bytes 98304 | tf_op jit(solution)/shard_map/all_gather | solution.py:61
  4.8 2.8 %gather_fusion.1 = bf16[256,256]{1,0:T(8,128)(2,1)S(1)} fusion(bf16[2,1024,256]{2,1,0:T(8,128)(2,1)} %param.7, s32[256]{0:T(256)S(1)} %fusion.28), kind=kCustom, calls=%fused_computation.1 | custom fusion | bytes 264192 | tf_op jit(solution)/shard_map/vmap()/gather | solution.py:66
  7.6 0.0 copy-done
  7.6 0.2 fusion.2
  7.8 0.0 collective-permute-done
  7.8 1.7 %gather_fusion = bf16[256,256]{1,0:T(8,128)(2,1)S(1)} fusion(bf16[2,128,256]{2,1,0:T(8,128)(2,1)S(1)} %collective-permute-done, s32[256]{0:T(256)S(1)} %fusion.29), kind=kCustom, calls=%fused_computation | custom fusion | bytes 264192 | tf_op jit(solution)/shard_map/vmap()/gather | solution.py:66
  9.4 0.1 broadcast_select_fusion
  9.5 0.2 fusion.1
  9.7 0.4 %select_reduce_fusion = (f32[2,64]{1,0:T(2,128)S(1)}, f32[2,64,128]{2,1,0:T(8,128)S(1)}) fusion(pred[2,128]{1,0:T(4,128)(4,1)S(1)} %bitcast.53, f32[2,64,128]{2,1,0:T(8,128)S(1)} %fusion.1, bf16[2,64,64]{2,1,0:T(8,128)(2,1)S(1)} %fusion.2, bf16[2,128,256]{2,1,0:T(8,128)(2,1)S(1)} %broadcast_select_fusion, bf16[256,64]{0,1:T(8,128)(2,1)S(1)} %copy-done), kind=kOutput, calls=%fused_computation.26 | convolution fusion | flops 10567552 | bytes 312064 | tf_op jit(solution)/shard_map/ucb,ukb->uck/dot_general | solution.py:75
  10.1 0.2 fusion.12
  10.3 0.2 fusion.11
  10.5 0.1 copy.13
  10.7 0.2 broadcast_in_dim.52
  10.9 0.1 reshape.90
  11.0 0.3 %collective-permute-start.1 = (f32[2,64,384]{2,1,0:T(8,128)S(1)}, f32[2,64,384]{2,1,0:T(8,128)S(1)}, u32[]{:S(2)}, u32[]{:S(2)}) collective-permute-start(f32[2,64,384]{2,1,0:T(8,128)S(1)} %pad_maximum_fusion), channel_id=1, source_target_pairs={{0,1},{1,0},{2,3},{3,2},{4,5},{5,4},{6,7},{7,6},{8,9},{9,8},{10,11... | collective-permute-start | bytes 589832 | tf_op jit(solution)/shard_map/ppermute | solution.py:41
  11.3 1.2 %collective-permute-done.1 = f32[2,64,384]{2,1,0:T(8,128)S(1)} collective-permute-done((f32[2,64,384]{2,1,0:T(8,128)S(1)}, f32[2,64,384]{2,1,0:T(8,128)S(1)}, u32[]{:S(2)}, u32[]{:S(2)}) %collective-permute-start.1) | collective-permute-done | bytes 196640 | tf_op jit(solution)/shard_map/ppermute | solution.py:41
  12.5 0.2 fusion.21
  12.7 0.0 copy-start.4
  12.7 0.1 fusion.32
  12.9 2.7 %collective-permute-start.2 = (f32[2,256]{1,0:T(2,128)S(1)}, f32[2,256]{1,0:T(2,128)S(1)}, u32[]{:S(2)}, u32[]{:S(2)}) collective-permute-start(f32[2,256]{1,0:T(2,128)S(1)} %pad_maximum_fusion.2), channel_id=1, source_target_pairs={{0,3},{1,2},{2,1},{3,0},{4,7},{5,6},{6,5},{7,4},{8,11},{9,10},{10,... | collective-permute-start | bytes 6152 | tf_op jit(solution)/shard_map/ppermute | solution.py:33
  15.6 1.3 %collective-permute-done.2 = f32[2,256]{1,0:T(2,128)S(1)} collective-permute-done((f32[2,256]{1,0:T(2,128)S(1)}, f32[2,256]{1,0:T(2,128)S(1)}, u32[]{:S(2)}, u32[]{:S(2)}) %collective-permute-start.2) | collective-permute-done | bytes 2080 | tf_op jit(solution)/shard_map/ppermute | solution.py:33
  16.9 1.8 %collective-permute-start.3 = (f32[2,256]{1,0:T(2,128)S(1)}, f32[2,256]{1,0:T(2,128)S(1)}, u32[]{:S(2)}, u32[]{:S(2)}) collective-permute-start(f32[2,256]{1,0:T(2,128)S(1)} %fusion.31), channel_id=1, source_target_pairs={{0,5},{1,4},{2,7},{3,6},{4,1},{5,0},{6,3},{7,2},{8,13},{9,12},{10,... | collective-permute-start | bytes 6152 | tf_op jit(solution)/shard_map/ppermute | solution.py:33
  18.7 1.3 %collective-permute-done.3 = f32[2,256]{1,0:T(2,128)S(1)} collective-permute-done((f32[2,256]{1,0:T(2,128)S(1)}, f32[2,256]{1,0:T(2,128)S(1)}, u32[]{:S(2)}, u32[]{:S(2)}) %collective-permute-start.3) | collective-permute-done | bytes 2080 | tf_op jit(solution)/shard_map/ppermute | solution.py:33
  20.0 2.0 %collective-permute-start.4 = (f32[2,256]{1,0:T(2,128)S(1)}, f32[2,256]{1,0:T(2,128)S(1)}, u32[]{:S(2)}, u32[]{:S(2)}) collective-permute-start(f32[2,256]{1,0:T(2,128)S(1)} %fusion.42), channel_id=1, source_target_pairs={{0,9},{1,8},{2,11},{3,10},{4,13},{5,12},{6,15},{7,14},{8,1},{9,0},... | collective-permute-start | bytes 6152 | tf_op jit(solution)/shard_map/ppermute | solution.py:33
  22.0 1.3 %collective-permute-done.4 = f32[2,256]{1,0:T(2,128)S(1)} collective-permute-done((f32[2,256]{1,0:T(2,128)S(1)}, f32[2,256]{1,0:T(2,128)S(1)}, u32[]{:S(2)}, u32[]{:S(2)}) %collective-permute-start.4) | collective-permute-done | bytes 2080 | tf_op jit(solution)/shard_map/ppermute | solution.py:33
  23.3 2.5 %collective-permute-start.5 = (f32[2,256]{1,0:T(2,128)S(1)}, f32[2,256]{1,0:T(2,128)S(1)}, u32[]{:S(2)}, u32[]{:S(2)}) collective-permute-start(f32[2,256]{1,0:T(2,128)S(1)} %add.94), channel_id=1, source_target_pairs={{0,17},{1,16},{2,19},{3,18},{4,21},{5,20},{6,23},{7,22},{8,25},{9,... | collective-permute-start | bytes 6152 | tf_op jit(solution)/shard_map/ppermute | solution.py:33
  25.8 1.4 %collective-permute-done.5 = f32[2,256]{1,0:T(2,128)S(1)} collective-permute-done((f32[2,256]{1,0:T(2,128)S(1)}, f32[2,256]{1,0:T(2,128)S(1)}, u32[]{:S(2)}, u32[]{:S(2)}) %collective-permute-start.5) | collective-permute-done | bytes 2080 | tf_op jit(solution)/shard_map/ppermute | solution.py:33
  27.2 0.0 copy-start.3
  27.2 0.0 copy-done.4
  27.3 0.7 %copy-done.3 = f32[256]{0:T(256)S(1)} copy-done((f32[256]{0:T(256)S(1)}, f32[256]{0:T(256)}, u32[]{:S(2)}) %copy-start.3) | copy-done | bytes 1048
  27.9 0.6 %add_convert_fusion = bf16[2,32,256]{2,1,0:T(8,128)(2,1)} fusion(f32[2,64,256]{2,1,0:T(8,128)S(1)} %get-tuple-element.10, s32[]{:T(128)S(6)} %select_n.39, f32[256]{0:T(256)S(1)} %copy-done.3, f32[256]{0:T(256)S(1)} %copy-done.4, f32[256]{0:T(256)S(1)} %add_rsqrt_fusion, f32[256]{0:T(256)S(1)} %bitcast.51), kind=kLoop, calls=%fused_computation.24 | loop fusion | flops 81920 | bytes 102404 | tf_op jit(solution)/shard_map/convert_element_type | solution.py:109
  (15 shorter events, 0.1 us)
Async XLA Ops:
  0.0 7.6 %copy-start = (bf16[256,64]{0,1:T(8,128)(2,1)S(1)}, bf16[256,64]{0,1:T(8,128)(2,1)}, u32[]{:S(2)}) copy-start(bf16[256,64]{0,1:T(8,128)(2,1)} %param.11) | copy-start | bytes 98308
  0.0 2.9 %copy-start.1 = (bf16[2,32,256]{2,1,0:T(8,128)(2,1)S(1)}, bf16[2,32,256]{2,1,0:T(8,128)(2,1)}, u32[]{:S(2)}) copy-start(bf16[2,32,256]{2,1,0:T(8,128)(2,1)} %param.8) | copy-start | bytes 98308
  0.9 6.8 %collective-permute-start = (bf16[2,128,256]{2,1,0:T(8,128)(2,1)S(1)}, bf16[2,128,256]{2,1,0:T(8,128)(2,1)S(1)}, u32[]{:S(2)}, u32[]{:S(2)}) collective-permute-start(bf16[2,128,256]{2,1,0:T(8,128)(2,1)S(1)} %slice.24), channel_id=1, source_target_pairs={{0,1},{1,0},{2,3},{3,2},{4,5},{5,4},{6,7},{7,6},{8,9},{9,8},{10,11... | collective-permute-start | bytes 393224 | tf_op jit(solution)/shard_map/ppermute | solution.py:60
  1.5 0.7 %copy-start.2 = (s32[2,1,128]{2,1,0:T(1,128)S(1)}, s32[2,1,128]{2,1,0:T(1,128)}, u32[]{:S(2)}) copy-start(s32[2,1,128]{2,1,0:T(1,128)} %param.9) | copy-start | bytes 3076
  2.2 0.7 %copy-start.5 = (s32[2]{0:T(128)S(1)}, s32[2]{0:T(128)}, u32[]{:S(2)}) copy-start(s32[2]{0:T(128)} %param.10) | copy-start | bytes 28
  11.0 1.5 %collective-permute-start.1 = (f32[2,64,384]{2,1,0:T(8,128)S(1)}, f32[2,64,384]{2,1,0:T(8,128)S(1)}, u32[]{:S(2)}, u32[]{:S(2)}) collective-permute-start(f32[2,64,384]{2,1,0:T(8,128)S(1)} %pad_maximum_fusion), channel_id=1, source_target_pairs={{0,1},{1,0},{2,3},{3,2},{4,5},{5,4},{6,7},{7,6},{8,9},{9,8},{10,11... | collective-permute-start | bytes 589832 | tf_op jit(solution)/shard_map/ppermute | solution.py:41
  12.7 14.5 %copy-start.4 = (f32[256]{0:T(256)S(1)}, f32[256]{0:T(256)}, u32[]{:S(2)}) copy-start(f32[256]{0:T(256)} %param.12) | copy-start | bytes 3076
  12.9 4.0 %collective-permute-start.2 = (f32[2,256]{1,0:T(2,128)S(1)}, f32[2,256]{1,0:T(2,128)S(1)}, u32[]{:S(2)}, u32[]{:S(2)}) collective-permute-start(f32[2,256]{1,0:T(2,128)S(1)} %pad_maximum_fusion.2), channel_id=1, source_target_pairs={{0,3},{1,2},{2,1},{3,0},{4,7},{5,6},{6,5},{7,4},{8,11},{9,10},{10,... | collective-permute-start | bytes 6152 | tf_op jit(solution)/shard_map/ppermute | solution.py:33
  16.9 3.1 %collective-permute-start.3 = (f32[2,256]{1,0:T(2,128)S(1)}, f32[2,256]{1,0:T(2,128)S(1)}, u32[]{:S(2)}, u32[]{:S(2)}) collective-permute-start(f32[2,256]{1,0:T(2,128)S(1)} %fusion.31), channel_id=1, source_target_pairs={{0,5},{1,4},{2,7},{3,6},{4,1},{5,0},{6,3},{7,2},{8,13},{9,12},{10,... | collective-permute-start | bytes 6152 | tf_op jit(solution)/shard_map/ppermute | solution.py:33
  20.0 3.3 %collective-permute-start.4 = (f32[2,256]{1,0:T(2,128)S(1)}, f32[2,256]{1,0:T(2,128)S(1)}, u32[]{:S(2)}, u32[]{:S(2)}) collective-permute-start(f32[2,256]{1,0:T(2,128)S(1)} %fusion.42), channel_id=1, source_target_pairs={{0,9},{1,8},{2,11},{3,10},{4,13},{5,12},{6,15},{7,14},{8,1},{9,0},... | collective-permute-start | bytes 6152 | tf_op jit(solution)/shard_map/ppermute | solution.py:33
  23.3 3.9 %collective-permute-start.5 = (f32[2,256]{1,0:T(2,128)S(1)}, f32[2,256]{1,0:T(2,128)S(1)}, u32[]{:S(2)}, u32[]{:S(2)}) collective-permute-start(f32[2,256]{1,0:T(2,128)S(1)} %add.94), channel_id=1, source_target_pairs={{0,17},{1,16},{2,19},{3,18},{4,21},{5,20},{6,23},{7,22},{8,25},{9,... | collective-permute-start | bytes 6152 | tf_op jit(solution)/shard_map/ppermute | solution.py:33
  27.2 0.7 %copy-start.3 = (f32[256]{0:T(256)S(1)}, f32[256]{0:T(256)}, u32[]{:S(2)}) copy-start(f32[256]{0:T(256)} %param.13) | copy-start | bytes 3076

commit v2 on v1

--- a/solution.py
+++ b/solution.py
@@ -3,6 +3,8 @@
 import jax
 import jax.numpy as jnp
 from jax import lax
+from jax.experimental import pallas as pl
+from jax.experimental.pallas import tpu as pltpu
 from jax.sharding import PartitionSpec as P
 
 HALO = 128
@@ -13,10 +15,9 @@
 NORM_EPS = 1e-05
 
 BOTH = ("user", "seq")
-
-
-def swapped_index(seq_index, seq_count):
-    return seq_index ^ 1 if seq_count % 2 == 0 else seq_index
+SIDE = 128
+CHUNK = 256
+VMEM_LIMIT = 8 * 1024 * 1024
 
 
 def user_total(value):
@@ -26,7 +27,7 @@
     stride = 1
     while stride < users:
         pairs = [
-            (user * seqs + seq, (user ^ stride) * seqs + swapped_index(seq, seqs))
+            (user * seqs + seq, (user ^ stride) * seqs + (seq ^ 1 if seqs % 2 == 0 else seq))
             for user in range(users)
             for seq in range(seqs)
         ]
@@ -35,12 +36,10 @@
     return value
 
 
-def seq_parts(value):
-    seqs = lax.axis_size("seq")
-    if seqs == 2:
-        return [value, lax.ppermute(value, "seq", [(0, 1), (1, 0)])]
-    everything = lax.all_gather(value, "seq")
-    return [everything[k] for k in range(seqs)]
+def last_with_last(left, right):
+    return lax.dot_general(
+        left, right, (((1,), (1,)), ((), ())), preferred_element_type=jnp.float32
+    )
 
 
 def soft_codes(rows, hash_planes):
@@ -49,7 +48,14 @@
     )
 
 
-def shards(behaviors, candidates, ranks, lengths, hash_planes, norm_gain, norm_bias):
+def normalized(own, moments, row_count, norm_gain, norm_bias):
+    feature_mean = moments[0] / row_count
+    feature_var = moments[1] / row_count - feature_mean * feature_mean
+    normed = (own - feature_mean) * lax.rsqrt(feature_var + NORM_EPS) * norm_gain + norm_bias
+    return normed.astype(jnp.bfloat16)
+
+
+def any_groups(behaviors, candidates, ranks, lengths, hash_planes, norm_gain, norm_bias):
     group_rows = behaviors.shape[1]
     feature_width = behaviors.shape[2]
     own_cands = candidates.shape[1]
@@ -83,30 +89,190 @@
     group_sum = jnp.einsum(
         "uck,ukd->ucd", weights.astype(jnp.bfloat16), picked, preferred_element_type=jnp.float32
     )
-    cands = group_sum.shape[1]
-    side = jnp.broadcast_to(
-        jnp.stack([group_max, group_total], axis=2)[..., None], group_sum.shape[:2] + (2, 64)
-    ).reshape(group_sum.shape[:2] + (128,))
-    parts = seq_parts(jnp.concatenate([group_sum, side], axis=2))
-    tops = [part[:, :, feature_width] for part in parts]
-    joint_max = tops[0]
-    for top in tops[1:]:
-        joint_max = jnp.maximum(joint_max, top)
-    numerator, denominator = 0.0, 0.0
-    for part, top in zip(parts, tops):
-        rescale = jnp.exp(top - joint_max)
-        numerator = numerator + rescale[..., None] * part[:, :, :feature_width]
-        denominator = denominator + rescale * part[:, :, feature_width + 64]
+    tops = lax.all_gather(group_max, "seq")
+    rescales = jnp.exp(tops - jnp.max(tops, axis=0))
+    numerator = jnp.sum(rescales[..., None] * lax.all_gather(group_sum, "seq"), axis=0)
+    denominator = jnp.sum(rescales * lax.all_gather(group_total, "seq"), axis=0)
     attended = numerator / denominator[..., None]
     moments = user_total(
         jnp.stack([jnp.sum(attended, axis=(0, 1)), jnp.sum(attended * attended, axis=(0, 1))])
     )
-    row_count = attended.shape[0] * cands * lax.axis_size("user")
-    feature_mean = moments[0] / row_count
-    feature_var = moments[1] / row_count - feature_mean * feature_mean
+    row_count = attended.shape[0] * attended.shape[1] * lax.axis_size("user")
     own = lax.dynamic_slice_in_dim(attended, seq_index * own_cands, own_cands, 1)
-    normed = (own - feature_mean) * lax.rsqrt(feature_var + NORM_EPS) * norm_gain + norm_bias
-    return normed.astype(jnp.bfloat16)
+    return normalized(own, moments, row_count, norm_gain, norm_bias)
+
+
+def rank_columns(rank_row, picks):
+    return jnp.transpose(jnp.broadcast_to(rank_row, (picks, picks)))
+
+
+def own_picks_kernel(
+    ranks_ref, lengths_ref, norm_gain_ref, norm_bias_ref, behaviors_hbm,
+    picked_ref, live_ref, gain_ref, bias_ref,
+    rows, row_sem,
+):
+    users, group_rows, _ = behaviors_hbm.shape
+    picks = ranks_ref.shape[2]
+    chunks = group_rows // CHUNK
+    loads = []
+    for user in range(users):
+        for chunk in range(chunks):
+            part = (user, pl.ds(chunk * CHUNK, CHUNK))
+            loads.append(
+                pltpu.make_async_copy(
+                    behaviors_hbm.at[part], rows.at[part], row_sem.at[user * chunks + chunk]
+                )
+            )
+            loads[-1].start()
+    start = lax.axis_index("seq") * group_rows - HALO
+    gain_ref[...] = norm_gain_ref[...]
+    bias_ref[...] = norm_bias_ref[...]
+    lanes = lax.broadcasted_iota(jnp.int32, (picks, CHUNK), 1)
+    for user in range(users):
+        position = ranks_ref[user] + start
+        usable = (position >= 0) & (position < lengths_ref[user])
+        live_ref[user] = usable.astype(jnp.float32)
+        columns = rank_columns(ranks_ref[user], picks)
+        wide = jnp.concatenate([columns] * (CHUNK // picks), axis=1) - HALO
+        found = jnp.zeros((picks, rows.shape[2]), jnp.float32)
+        for chunk in range(chunks):
+            loads[user * chunks + chunk].wait()
+            chosen = (wide == lanes + chunk * CHUNK).astype(jnp.float32).astype(jnp.bfloat16)
+            found += jnp.dot(
+                chosen,
+                rows[user, chunk * CHUNK : (chunk + 1) * CHUNK],
+                preferred_element_type=jnp.float32,
+            )
+        picked_ref[user] = found.astype(jnp.bfloat16)
+
+
+def attend_kernel(ranks_ref, live_ref, picked_ref, mine_ref, other_ref, planes_ref, part_ref):
+    users, picks, feature_width = picked_ref.shape
+    code_bits = planes_ref.shape[0]
+    planes = planes_ref[...]
+    lanes = lax.broadcasted_iota(jnp.int32, (picks, HALO), 1)
+    for user in range(users):
+        chosen = rank_columns(ranks_ref[user], picks) == lanes
+        from_tail = jnp.dot(
+            chosen.astype(jnp.float32).astype(jnp.bfloat16),
+            other_ref[user, :HALO],
+            preferred_element_type=jnp.float32,
+        )
+        picked = (picked_ref[user].astype(jnp.float32) + from_tail).astype(jnp.bfloat16)
+        queries = jnp.concatenate([mine_ref[user], other_ref[user, HALO:]], axis=0)
+        query_codes = jnp.tanh(last_with_last(queries, planes)).astype(jnp.bfloat16)
+        picked_codes = jnp.tanh(last_with_last(picked, planes)).astype(jnp.bfloat16)
+        similar = last_with_last(queries, picked)
+        agreement = last_with_last(query_codes, picked_codes)
+        scores = similar * (1.0 / math.sqrt(feature_width)) + HASH_WEIGHT / code_bits * agreement
+        usable = live_ref[user] > 0.0
+        group_max = jnp.max(jnp.where(usable, scores, NEG_FILL), axis=1, keepdims=True)
+        weights = jnp.where(usable, jnp.exp(scores - group_max), 0.0)
+        group_total = jnp.sum(weights, axis=1, keepdims=True)
+        part_ref[user, :, :feature_width] = jnp.dot(
+            weights.astype(jnp.bfloat16), picked, preferred_element_type=jnp.float32
+        )
+        side_lane = lax.broadcasted_iota(jnp.int32, (queries.shape[0], SIDE), 1)
+        part_ref[user, :, feature_width:] = jnp.where(
+            side_lane < SIDE // 2, group_max, group_total
+        )
+
+
+def merge_kernel(mine_ref, other_ref, own_ref, moments_ref):
+    users, cands, packed = mine_ref.shape
+    width = packed - SIDE
+    half = cands // 2
+    sums = jnp.zeros((1, width), jnp.float32)
+    squares = jnp.zeros((1, width), jnp.float32)
+    for user in range(users):
+        for first in (0, half):
+            left = mine_ref[user, first : first + half]
+            right = other_ref[user, half - first : cands - first]
+            left_top, right_top = left[:, width : width + 1], right[:, width : width + 1]
+            last = width + SIDE // 2
+            joint_max = jnp.maximum(left_top, right_top)
+            left_scale = jnp.exp(left_top - joint_max)
+            right_scale = jnp.exp(right_top - joint_max)
+            numerator = left_scale * left[:, :width] + right_scale * right[:, :width]
+            denominator = (
+                left_scale * left[:, last : last + 1] + right_scale * right[:, last : last + 1]
+            )
+            attended = numerator / denominator
+            sums += jnp.sum(attended, axis=0, keepdims=True)
+            squares += jnp.sum(attended * attended, axis=0, keepdims=True)
+            if first == 0:
+                own_ref[user] = attended
+    moments_ref[0:1] = sums
+    moments_ref[1:2] = squares
+
+
+def two_groups(behaviors, candidates, ranks, lengths, hash_planes, norm_gain, norm_bias):
+    users, group_rows, width = behaviors.shape
+    own_cands = candidates.shape[1]
+    picks = ranks.shape[2]
+    cands = 2 * own_cands
+    f32, bf16 = jnp.float32, jnp.bfloat16
+    in_vmem = pl.BlockSpec(memory_space=pltpu.VMEM)
+    swap = [(0, 1), (1, 0)]
+    other = lax.ppermute(
+        jnp.concatenate([behaviors[:, group_rows - HALO :], candidates], axis=1), "seq", swap
+    )
+    loads = users * group_rows // CHUNK
+    picked, live, gain, bias = pl.pallas_call(
+        own_picks_kernel,
+        out_shape=(
+            jax.ShapeDtypeStruct((users, picks, width), bf16),
+            jax.ShapeDtypeStruct((users, 1, picks), f32),
+            jax.ShapeDtypeStruct(norm_gain.shape, f32),
+            jax.ShapeDtypeStruct(norm_bias.shape, f32),
+        ),
+        in_specs=[
+            in_vmem,
+            pl.BlockSpec(memory_space=pltpu.SMEM),
+            in_vmem,
+            in_vmem,
+            pl.BlockSpec(memory_space=pl.ANY),
+        ],
+        out_specs=(in_vmem,) * 4,
+        scratch_shapes=[
+            pltpu.VMEM(behaviors.shape, bf16),
+            pltpu.SemaphoreType.DMA((loads,)),
+        ],
+        cost_estimate=pl.CostEstimate(
+            flops=2 * users * picks * group_rows * width,
+            bytes_accessed=behaviors.nbytes,
+            transcendentals=0,
+        ),
+        compiler_params=pltpu.CompilerParams(vmem_limit_bytes=VMEM_LIMIT),
+        name="own_picks",
+    )(
+        ranks,
+        lengths,
+        norm_gain,
+        norm_bias,
+        pltpu.with_memory_space_constraint(behaviors, pltpu.HBM),
+    )
+    part = pl.pallas_call(
+        attend_kernel,
+        out_shape=jax.ShapeDtypeStruct((users, cands, width + SIDE), f32),
+        in_specs=[in_vmem] * 6,
+        out_specs=in_vmem,
+        compiler_params=pltpu.CompilerParams(vmem_limit_bytes=VMEM_LIMIT),
+        name="attend",
+    )(ranks, live, picked, candidates, other, hash_planes.T)
+    own, moments = pl.pallas_call(
+        merge_kernel,
+        out_shape=(
+            jax.ShapeDtypeStruct((users, own_cands, width), f32),
+            jax.ShapeDtypeStruct((2, width), f32),
+        ),
+        in_specs=[in_vmem] * 2,
+        out_specs=(in_vmem,) * 2,
+        compiler_params=pltpu.CompilerParams(vmem_limit_bytes=VMEM_LIMIT),
+        name="merge",
+    )(part, lax.ppermute(part, "seq", swap))
+    row_count = users * cands * lax.axis_size("user")
+    return normalized(own, user_total(moments), row_count, gain, bias)
 
 
 def solution(mesh):
@@ -120,4 +286,5 @@
         P(),
     )
     out_specs = P("user", "seq", None)
+    shards = two_groups if mesh.shape["seq"] == 2 else any_groups
     return jax.shard_map(shards, mesh=mesh, in_specs=in_specs, out_specs=out_specs, check_vma=False)

time: 28.8 us -> 22 us (0.76)
  local copies, waits for them, and re-layouts: 7.8 us -> 1.02 us
  Pallas kernels: 0 us -> 3.71 us
  blocking collectives: 1.85 us -> 0 us
  matrix products: 0.96 us -> 0 us
  other arithmetic: 1.41 us -> 0.68 us
    gather x2 -> x0, local copies, waits for them, and re-layouts: 4.41 us -> none  [shards(): take_rows = jax.vmap(lambda row_table, where_at: row_table[where_at])]
    pallas_call x0 -> x3, Pallas kernels: none -> 3.71 us  [the longest x1 2.3 us: two_groups(): pl.pallas_call(own_picks_kernel, out_shape=(jax.ShapeDtypeStruct((users,...]
    unnamed x14 -> x12, local copies, waits for them, and re-layouts: 2.02 us -> 0.12 us
    all_gather x1 -> x0, blocking collectives: 1.85 us -> none  [shards(): queries = lax.all_gather(candidates, 'seq', axis=1, tiled=True)]
    dot_general x4 -> x0, matrix products: 0.96 us -> none  [the longest x1 0.42 us: shards(): jnp.einsum('ucb,ukb->uck', query_codes, picked_codes, preferred_element_t...]
    reduce_sum x2 -> x0, other arithmetic: 0.32 us -> none  [the longest x1 0.18 us: shards(): group_total = jnp.sum(weights, axis=2)]
    slice x1 -> x2, local copies, waits for them, and re-layouts: 0.93 us -> 0.9 us  [two_groups(): behaviors[:, group_rows - HALO:]]
  transfers between devices with their start and end apart: 6 -> 6, of which waited for: 5 -> 5; matrix products, arithmetic and copies ran while one was open for 11% -> 0% of each run, Pallas kernels for 0% -> 11%
where the time goes in v2:
time: 22 us; the launch traced here: 21.8 us
  starting transfers between devices  9.97 us (45%)
  waiting for transfers between devices  6.31 us (29%)
  Pallas kernels  3.71 us (17%)
  local copies, waits for them, and re-layouts  1.02 us (5%)
  other arithmetic  0.68 us (3%)
    ppermute x4, starting transfers between devices, user_total(): value = value + lax.ppermute(value, BOTH, pairs)  8.86 us
    ppermute x4, waiting for transfers between devices, user_total(): value = value + lax.ppermute(value, BOTH, pairs)  5.24 us
    pallas_call x1, Pallas kernels, two_groups(): pl.pallas_call(own_picks_kernel, out_shape=(jax.ShapeDtypeStruct((users,...  2.3 us
    pallas_call x1, Pallas kernels, two_groups(): pl.pallas_call(attend_kernel, out_shape=jax.ShapeDtypeStruct((users, cand...  1.19 us
    ppermute x1, waiting for transfers between devices, two_groups(): lax.ppermute(part, 'seq', swap)  1.07 us
    slice x2, local copies, waits for them, and re-layouts, two_groups(): behaviors[:, group_rows - HALO:]  0.9 us
    convert_element_type x1, other arithmetic, normalized(): return normed.astype(jnp.bfloat16)  0.63 us
    ppermute x1, starting transfers between devices, two_groups(): lax.ppermute(jnp.concatenate([behaviors[:, group_rows - HALO:], candidate...  0.56 us
  transfers between devices with their start and end apart: 6, of which 5 were waited for; matrix products, arithmetic and copies ran while one was open for 0% of the time, Pallas kernels for 11%

profile of v2, /device:TPU:0, one launch (start us, length us, event | category | flops | bytes accessed | tf_op | source)
XLA Modules:
  0.0 21.8 jit_solution(1369288421536044528)
XLA Ops:
  0.0 0.0 slice-start
  0.0 0.0 copy-start
  0.0 0.9 %slice-done = bf16[2,128,256]{2,1,0:T(8,128)(2,1)S(1)} async-done(((bf16[2,1024,256]{2,1,0:T(8,128)(2,1)}), bf16[2,128,256]{2,1,0:T(8,128)(2,1)S(1)}, s32[]{:S(2)}) %slice-start) | async-done | bytes 131096 | tf_op jit(solution)/shard_map/slice | solution.py:218
  0.9 0.0 copy-done
  0.9 0.0 copy-start.2
  0.9 0.0 copy-start.3
  0.9 0.0 copy-start.4
  0.9 0.0 copy-start.5
  0.9 0.0 copy-start.1
  1.0 0.6 %collective-permute-start = (bf16[2,160,256]{2,1,0:T(8,128)(2,1)S(1)}, bf16[2,160,256]{2,1,0:T(8,128)(2,1)S(1)}, u32[]{:S(2)}, u32[]{:S(2)}) collective-permute-start(bf16[2,160,256]{2,1,0:T(8,128)(2,1)S(1)} %pad_maximum_fusion), channel_id=1, source_target_pairs={{0,1},{1,0},{2,3},{3,2},{4,5},{5,4},{6,7},{7,6},{8,9},{9,8},{10,11... | collective-permute-start | bytes 491528 | tf_op jit(solution)/shard_map/ppermute | solution.py:217
  1.5 0.1 copy-done.2
  1.6 0.0 copy-done.3
  1.6 0.0 copy-done.4
  1.6 0.0 copy-done.5
  1.6 2.3 %own_picks.1 = (bf16[2,128,256]{2,1,0:T(8,128)(2,1)S(1)}, f32[2,1,128]{2,1,0:T(1,128)S(1)}, f32[256]{0:T(256)S(1)}, f32[256]{0:T(256)S(1)}) custom-call(s32[2,1,128]{2,1,0:T(1,128)S(1)} %copy-done.2, s32[2]{0:T(128)S(1)} %copy-done.5, f32[256]{0:T(256)S(1)} %copy-done.3, f32[256]{0:T(256)S(1)} %copy-done.4, bf16[2,1024,256]{2,1,0:T(8,128)(2,1)} %behaviors_hbm.1), custom_call_target="tpu_custom_call" | custom-call | flops 134217728 | bytes 1048576 | tf_op jit(solution)/shard_map/own_picks/pallas_call | solution.py:221
  3.9 0.0 collective-permute-done.other_ref
  3.9 0.0 copy-done.1
  4.0 1.2 %attend.1.mine_ref = f32[2,64,384]{2,1,0:T(8,128)S(1)} custom-call(s32[2,1,128]{2,1,0:T(1,128)S(1)} %copy-done.2, f32[2,1,128]{2,1,0:T(1,128)S(1)} %get-tuple-element.11.live_ref, bf16[2,128,256]{2,1,0:T(8,128)(2,1)S(1)} %get-tuple-element.12.picked_ref, bf16[2,32,256]{2,1,0:T(8,128)(2,1)S(1)} %copy-done, ...), custom_call_target="tpu_custom_call" | custom-call | tf_op jit(solution)/shard_map/attend/pallas_call | solution.py:255
  5.1 0.6 %collective-permute-start.1 = (f32[2,64,384]{2,1,0:T(8,128)S(1)}, f32[2,64,384]{2,1,0:T(8,128)S(1)}, u32[]{:S(2)}, u32[]{:S(2)}) collective-permute-start(f32[2,64,384]{2,1,0:T(8,128)S(1)} %attend.1.mine_ref), channel_id=1, source_target_pairs={{0,1},{1,0},{2,3},{3,2},{4,5},{5,4},{6,7},{7,6},{8,9},{9,8},{10,11... | collective-permute-start | bytes 589832 | tf_op jit(solution)/shard_map/ppermute | solution.py:273
  5.7 1.1 %collective-permute-done.1.other_ref = f32[2,64,384]{2,1,0:T(8,128)S(1)} collective-permute-done((f32[2,64,384]{2,1,0:T(8,128)S(1)}, f32[2,64,384]{2,1,0:T(8,128)S(1)}, u32[]{:S(2)}, u32[]{:S(2)}) %collective-permute-start.1) | collective-permute-done | bytes 196640 | tf_op jit(solution)/shard_map/ppermute | solution.py:273
  6.8 0.2 %merge.1 = (f32[2,32,256]{2,1,0:T(8,128)S(1)}, f32[2,256]{1,0:T(2,128)S(1)}) custom-call(f32[2,64,384]{2,1,0:T(8,128)S(1)} %attend.1.mine_ref, f32[2,64,384]{2,1,0:T(8,128)S(1)} %collective-permute-done.1.other_ref), custom_call_target="tpu_custom_call" | custom-call | tf_op jit(solution)/shard_map/merge/pallas_call | solution.py:263
  7.0 2.6 %collective-permute-start.2 = (f32[2,256]{1,0:T(2,128)S(1)}, f32[2,256]{1,0:T(2,128)S(1)}, u32[]{:S(2)}, u32[]{:S(2)}) collective-permute-start(f32[2,256]{1,0:T(2,128)S(1)} %get-tuple-element.14), channel_id=1, source_target_pairs={{0,3},{1,2},{2,1},{3,0},{4,7},{5,6},{6,5},{7,4},{8,11},{9,10},{10,... | collective-permute-start | bytes 6152 | tf_op jit(solution)/shard_map/ppermute | solution.py:34
  9.7 1.3 %collective-permute-done.2 = f32[2,256]{1,0:T(2,128)S(1)} collective-permute-done((f32[2,256]{1,0:T(2,128)S(1)}, f32[2,256]{1,0:T(2,128)S(1)}, u32[]{:S(2)}, u32[]{:S(2)}) %collective-permute-start.2) | collective-permute-done | bytes 2080 | tf_op jit(solution)/shard_map/ppermute | solution.py:34
  11.0 1.7 %collective-permute-start.3 = (f32[2,256]{1,0:T(2,128)S(1)}, f32[2,256]{1,0:T(2,128)S(1)}, u32[]{:S(2)}, u32[]{:S(2)}) collective-permute-start(f32[2,256]{1,0:T(2,128)S(1)} %add.30), channel_id=1, source_target_pairs={{0,5},{1,4},{2,7},{3,6},{4,1},{5,0},{6,3},{7,2},{8,13},{9,12},{10,... | collective-permute-start | bytes 6152 | tf_op jit(solution)/shard_map/ppermute | solution.py:34
  12.7 1.3 %collective-permute-done.3 = f32[2,256]{1,0:T(2,128)S(1)} collective-permute-done((f32[2,256]{1,0:T(2,128)S(1)}, f32[2,256]{1,0:T(2,128)S(1)}, u32[]{:S(2)}, u32[]{:S(2)}) %collective-permute-start.3) | collective-permute-done | bytes 2080 | tf_op jit(solution)/shard_map/ppermute | solution.py:34
  14.0 1.8 %collective-permute-start.4 = (f32[2,256]{1,0:T(2,128)S(1)}, f32[2,256]{1,0:T(2,128)S(1)}, u32[]{:S(2)}, u32[]{:S(2)}) collective-permute-start(f32[2,256]{1,0:T(2,128)S(1)} %add.31), channel_id=1, source_target_pairs={{0,9},{1,8},{2,11},{3,10},{4,13},{5,12},{6,15},{7,14},{8,1},{9,0},... | collective-permute-start | bytes 6152 | tf_op jit(solution)/shard_map/ppermute | solution.py:34
  15.8 1.3 %collective-permute-done.4 = f32[2,256]{1,0:T(2,128)S(1)} collective-permute-done((f32[2,256]{1,0:T(2,128)S(1)}, f32[2,256]{1,0:T(2,128)S(1)}, u32[]{:S(2)}, u32[]{:S(2)}) %collective-permute-start.4) | collective-permute-done | bytes 2080 | tf_op jit(solution)/shard_map/ppermute | solution.py:34
  17.1 2.7 %collective-permute-start.5 = (f32[2,256]{1,0:T(2,128)S(1)}, f32[2,256]{1,0:T(2,128)S(1)}, u32[]{:S(2)}, u32[]{:S(2)}) collective-permute-start(f32[2,256]{1,0:T(2,128)S(1)} %add.32), channel_id=1, source_target_pairs={{0,17},{1,16},{2,19},{3,18},{4,21},{5,20},{6,23},{7,22},{8,25},{9,... | collective-permute-start | bytes 6152 | tf_op jit(solution)/shard_map/ppermute | solution.py:34
  19.8 1.3 %collective-permute-done.5 = f32[2,256]{1,0:T(2,128)S(1)} collective-permute-done((f32[2,256]{1,0:T(2,128)S(1)}, f32[2,256]{1,0:T(2,128)S(1)}, u32[]{:S(2)}, u32[]{:S(2)}) %collective-permute-start.5) | collective-permute-done | bytes 2080 | tf_op jit(solution)/shard_map/ppermute | solution.py:34
  21.1 0.6 %add_convert_fusion = bf16[2,32,256]{2,1,0:T(8,128)(2,1)} fusion(f32[2,32,256]{2,1,0:T(8,128)S(1)} %get-tuple-element.13, f32[256]{0:T(256)S(1)} %get-tuple-element.16, f32[256]{0:T(256)S(1)} %get-tuple-element.15, f32[256]{0:T(256)S(1)} %add_rsqrt_fusion, f32[256]{0:T(256)S(1)} %bitcast.5), kind=kLoop, calls=%fused_computation.1 | loop fusion | flops 81920 | bytes 102400 | tf_op jit(solution)/shard_map/convert_element_type | solution.py:55
  (7 shorter events, 0.0 us)
Async XLA Ops:
  0.0 0.9 %slice-start = ((bf16[2,1024,256]{2,1,0:T(8,128)(2,1)}), bf16[2,128,256]{2,1,0:T(8,128)(2,1)S(1)}, s32[]{:S(2)}) async-start(bf16[2,1024,256]{2,1,0:T(8,128)(2,1)} %behaviors_hbm.1), calls=%async_computation | async-start | bytes 262144 | tf_op jit(solution)/shard_map/slice | solution.py:218
  0.0 0.9 %copy-start = (bf16[2,32,256]{2,1,0:T(8,128)(2,1)S(1)}, bf16[2,32,256]{2,1,0:T(8,128)(2,1)}, u32[]{:S(2)}) copy-start(bf16[2,32,256]{2,1,0:T(8,128)(2,1)} %mine_ref.1) | copy-start | bytes 98308
  0.9 0.7 %copy-start.2 = (s32[2,1,128]{2,1,0:T(1,128)S(1)}, s32[2,1,128]{2,1,0:T(1,128)}, u32[]{:S(2)}) copy-start(s32[2,1,128]{2,1,0:T(1,128)} %ranks_ref.3) | copy-start | bytes 3076
  0.9 0.7 %copy-start.3 = (f32[256]{0:T(256)S(1)}, f32[256]{0:T(256)}, u32[]{:S(2)}) copy-start(f32[256]{0:T(256)} %norm_gain_ref.1) | copy-start | bytes 3076
  0.9 0.7 %copy-start.4 = (f32[256]{0:T(256)S(1)}, f32[256]{0:T(256)}, u32[]{:S(2)}) copy-start(f32[256]{0:T(256)} %norm_bias_ref.1) | copy-start | bytes 3076
  0.9 0.7 %copy-start.5 = (s32[2]{0:T(128)S(1)}, s32[2]{0:T(128)}, u32[]{:S(2)}) copy-start(s32[2]{0:T(128)} %lengths_ref.1) | copy-start | bytes 28
  0.9 3.0 %copy-start.1 = (bf16[256,64]{0,1:T(8,128)(2,1)S(1)}, bf16[256,64]{0,1:T(8,128)(2,1)}, u32[]{:S(2)}) copy-start(bf16[256,64]{0,1:T(8,128)(2,1)} %param.11) | copy-start | bytes 98308
  1.0 3.0 %collective-permute-start = (bf16[2,160,256]{2,1,0:T(8,128)(2,1)S(1)}, bf16[2,160,256]{2,1,0:T(8,128)(2,1)S(1)}, u32[]{:S(2)}, u32[]{:S(2)}) collective-permute-start(bf16[2,160,256]{2,1,0:T(8,128)(2,1)S(1)} %pad_maximum_fusion), channel_id=1, source_target_pairs={{0,1},{1,0},{2,3},{3,2},{4,5},{5,4},{6,7},{7,6},{8,9},{9,8},{10,11... | collective-permute-start | bytes 491528 | tf_op jit(solution)/shard_map/ppermute | solution.py:217
  5.1 1.6 %collective-permute-start.1 = (f32[2,64,384]{2,1,0:T(8,128)S(1)}, f32[2,64,384]{2,1,0:T(8,128)S(1)}, u32[]{:S(2)}, u32[]{:S(2)}) collective-permute-start(f32[2,64,384]{2,1,0:T(8,128)S(1)} %attend.1.mine_ref), channel_id=1, source_target_pairs={{0,1},{1,0},{2,3},{3,2},{4,5},{5,4},{6,7},{7,6},{8,9},{9,8},{10,11... | collective-permute-start | bytes 589832 | tf_op jit(solution)/shard_map/ppermute | solution.py:273
  7.0 4.0 %collective-permute-start.2 = (f32[2,256]{1,0:T(2,128)S(1)}, f32[2,256]{1,0:T(2,128)S(1)}, u32[]{:S(2)}, u32[]{:S(2)}) collective-permute-start(f32[2,256]{1,0:T(2,128)S(1)} %get-tuple-element.14), channel_id=1, source_target_pairs={{0,3},{1,2},{2,1},{3,0},{4,7},{5,6},{6,5},{7,4},{8,11},{9,10},{10,... | collective-permute-start | bytes 6152 | tf_op jit(solution)/shard_map/ppermute | solution.py:34
  11.0 3.0 %collective-permute-start.3 = (f32[2,256]{1,0:T(2,128)S(1)}, f32[2,256]{1,0:T(2,128)S(1)}, u32[]{:S(2)}, u32[]{:S(2)}) collective-permute-start(f32[2,256]{1,0:T(2,128)S(1)} %add.30), channel_id=1, source_target_pairs={{0,5},{1,4},{2,7},{3,6},{4,1},{5,0},{6,3},{7,2},{8,13},{9,12},{10,... | collective-permute-start | bytes 6152 | tf_op jit(solution)/shard_map/ppermute | solution.py:34
  14.0 3.1 %collective-permute-start.4 = (f32[2,256]{1,0:T(2,128)S(1)}, f32[2,256]{1,0:T(2,128)S(1)}, u32[]{:S(2)}, u32[]{:S(2)}) collective-permute-start(f32[2,256]{1,0:T(2,128)S(1)} %add.31), channel_id=1, source_target_pairs={{0,9},{1,8},{2,11},{3,10},{4,13},{5,12},{6,15},{7,14},{8,1},{9,0},... | collective-permute-start | bytes 6152 | tf_op jit(solution)/shard_map/ppermute | solution.py:34
  17.1 4.0 %collective-permute-start.5 = (f32[2,256]{1,0:T(2,128)S(1)}, f32[2,256]{1,0:T(2,128)S(1)}, u32[]{:S(2)}, u32[]{:S(2)}) collective-permute-start(f32[2,256]{1,0:T(2,128)S(1)} %add.32), channel_id=1, source_target_pairs={{0,17},{1,16},{2,19},{3,18},{4,21},{5,20},{6,23},{7,22},{8,25},{9,... | collective-permute-start | bytes 6152 | tf_op jit(solution)/shard_map/ppermute | solution.py:34

commit v3 on v2

--- a/solution.py
+++ b/solution.py
@@ -16,7 +16,8 @@
 
 BOTH = ("user", "seq")
 SIDE = 128
-CHUNK = 256
+CHUNK = 1024
+TAIL_CHUNK = 128
 VMEM_LIMIT = 8 * 1024 * 1024
 
 
@@ -42,10 +43,8 @@
     )
 
 
-def soft_codes(rows, hash_planes):
-    return jnp.tanh(jnp.dot(rows, hash_planes, preferred_element_type=jnp.float32)).astype(
-        jnp.bfloat16
-    )
+def soft_codes(rows, planes):
+    return jnp.tanh(last_with_last(rows, planes)).astype(jnp.bfloat16)
 
 
 def normalized(own, moments, row_count, norm_gain, norm_bias):
@@ -75,8 +74,12 @@
     )
     position = seq_index * group_rows - HALO + window_pos
     usable = (position >= 0) & (position < lengths[:, None])
-    query_codes = soft_codes(queries, hash_planes)
-    picked_codes = soft_codes(picked, hash_planes)
+    query_codes, picked_codes = (
+        jnp.tanh(
+            jnp.einsum("ukd,db->ukb", rows, hash_planes, preferred_element_type=jnp.float32)
+        ).astype(jnp.bfloat16)
+        for rows in (queries, picked)
+    )
     similar = jnp.einsum("ucd,ukd->uck", queries, picked, preferred_element_type=jnp.float32)
     agreement = jnp.einsum(
         "ucb,ukb->uck", query_codes, picked_codes, preferred_element_type=jnp.float32
@@ -102,80 +105,100 @@
     return normalized(own, moments, row_count, norm_gain, norm_bias)
 
 
-def rank_columns(rank_row, picks):
-    return jnp.transpose(jnp.broadcast_to(rank_row, (picks, picks)))
-
-
-def own_picks_kernel(
-    ranks_ref, lengths_ref, norm_gain_ref, norm_bias_ref, behaviors_hbm,
-    picked_ref, live_ref, gain_ref, bias_ref,
-    rows, row_sem,
+def load_kernel(
+    ranks_hbm, lengths_hbm, norm_gain_hbm, norm_bias_hbm, planes_hbm, mine_hbm, behaviors_hbm,
+    sent_ref, rows_ref, mine_ref, places_ref, gain_ref, bias_ref, planes_ref,
+    ranks, lengths, sems,
 ):
     users, group_rows, _ = behaviors_hbm.shape
-    picks = ranks_ref.shape[2]
-    chunks = group_rows // CHUNK
-    loads = []
-    for user in range(users):
-        for chunk in range(chunks):
-            part = (user, pl.ds(chunk * CHUNK, CHUNK))
-            loads.append(
-                pltpu.make_async_copy(
-                    behaviors_hbm.at[part], rows.at[part], row_sem.at[user * chunks + chunk]
+    tail = group_rows - HALO
+    pairs = [
+        (ranks_hbm, ranks),
+        (lengths_hbm, lengths),
+        (planes_hbm, planes_ref),
+        (mine_hbm, mine_ref),
+        (mine_hbm, sent_ref.at[:, pl.ds(HALO, mine_ref.shape[1])]),
+        (norm_gain_hbm, gain_ref),
+        (norm_bias_hbm, bias_ref),
+    ]
+    for user in range(users):
+        for first in range(0, HALO, TAIL_CHUNK):
+            pairs.append(
+                (
+                    behaviors_hbm.at[user, pl.ds(tail + first, TAIL_CHUNK)],
+                    sent_ref.at[user, pl.ds(first, TAIL_CHUNK)],
                 )
             )
-            loads[-1].start()
+    for user in range(users):
+        for first in range(0, group_rows, CHUNK):
+            part = (user, pl.ds(first, CHUNK))
+            pairs.append((behaviors_hbm.at[part], rows_ref.at[part]))
+    copies = [
+        pltpu.make_async_copy(source, target, sems.at[k])
+        for k, (source, target) in enumerate(pairs)
+    ]
+    for copy in copies:
+        copy.start()
+    for copy in copies[:2]:
+        copy.wait()
     start = lax.axis_index("seq") * group_rows - HALO
-    gain_ref[...] = norm_gain_ref[...]
-    bias_ref[...] = norm_bias_ref[...]
-    lanes = lax.broadcasted_iota(jnp.int32, (picks, CHUNK), 1)
-    for user in range(users):
-        position = ranks_ref[user] + start
-        usable = (position >= 0) & (position < lengths_ref[user])
-        live_ref[user] = usable.astype(jnp.float32)
-        columns = rank_columns(ranks_ref[user], picks)
-        wide = jnp.concatenate([columns] * (CHUNK // picks), axis=1) - HALO
-        found = jnp.zeros((picks, rows.shape[2]), jnp.float32)
-        for chunk in range(chunks):
-            loads[user * chunks + chunk].wait()
-            chosen = (wide == lanes + chunk * CHUNK).astype(jnp.float32).astype(jnp.bfloat16)
-            found += jnp.dot(
-                chosen,
-                rows[user, chunk * CHUNK : (chunk + 1) * CHUNK],
-                preferred_element_type=jnp.float32,
-            )
-        picked_ref[user] = found.astype(jnp.bfloat16)
-
-
-def attend_kernel(ranks_ref, live_ref, picked_ref, mine_ref, other_ref, planes_ref, part_ref):
-    users, picks, feature_width = picked_ref.shape
+    for user in range(users):
+        position = ranks[user] + start
+        usable = (position >= 0) & (position < lengths[user])
+        places_ref[user] = jnp.where(usable, ranks[user], HALO + group_rows)
+    for copy in copies[2:]:
+        copy.wait()
+
+
+def own_picks_kernel(
+    places_ref, rows_ref, mine_ref, planes_ref,
+    picked_ref, picked_codes_ref, mine_codes_ref, masks_ref,
+):
+    users, group_rows, _ = rows_ref.shape
+    picks = places_ref.shape[2]
+    planes = planes_ref[...]
+    lanes = lax.broadcasted_iota(jnp.int32, (picks, group_rows), 1)
+    for user in range(users):
+        places = places_ref[user]
+        columns = jnp.transpose(jnp.broadcast_to(places, (picks, picks)))
+        in_tail = (columns == lanes[:, :HALO]).astype(jnp.float32)
+        masks_ref[user, 0:1] = ((places >= HALO) & (places < HALO + group_rows)).astype(jnp.float32)
+        masks_ref[user, 1:2] = jnp.max(in_tail, axis=0, keepdims=True)
+        wide = jnp.concatenate([columns - HALO] * (group_rows // picks), axis=1)
+        chosen = (wide == lanes).astype(jnp.float32).astype(jnp.bfloat16)
+        picked = jnp.dot(chosen, rows_ref[user], preferred_element_type=jnp.float32).astype(
+            jnp.bfloat16
+        )
+        picked_ref[user] = picked
+        picked_codes_ref[user] = soft_codes(picked, planes)
+        mine_codes_ref[user] = soft_codes(mine_ref[user], planes)
+
+
+def attend_kernel(
+    masks_ref, picked_ref, picked_codes_ref, mine_ref, mine_codes_ref, other_ref, planes_ref,
+    part_ref,
+):
+    users, _, width = picked_ref.shape
     code_bits = planes_ref.shape[0]
     planes = planes_ref[...]
-    lanes = lax.broadcasted_iota(jnp.int32, (picks, HALO), 1)
-    for user in range(users):
-        chosen = rank_columns(ranks_ref[user], picks) == lanes
-        from_tail = jnp.dot(
-            chosen.astype(jnp.float32).astype(jnp.bfloat16),
-            other_ref[user, :HALO],
-            preferred_element_type=jnp.float32,
-        )
-        picked = (picked_ref[user].astype(jnp.float32) + from_tail).astype(jnp.bfloat16)
+    for user in range(users):
+        codes = soft_codes(other_ref[user], planes)
         queries = jnp.concatenate([mine_ref[user], other_ref[user, HALO:]], axis=0)
-        query_codes = jnp.tanh(last_with_last(queries, planes)).astype(jnp.bfloat16)
-        picked_codes = jnp.tanh(last_with_last(picked, planes)).astype(jnp.bfloat16)
-        similar = last_with_last(queries, picked)
-        agreement = last_with_last(query_codes, picked_codes)
-        scores = similar * (1.0 / math.sqrt(feature_width)) + HASH_WEIGHT / code_bits * agreement
-        usable = live_ref[user] > 0.0
+        query_codes = jnp.concatenate([mine_codes_ref[user], codes[HALO:]], axis=0)
+        rows = jnp.concatenate([picked_ref[user], other_ref[user, :HALO]], axis=0)
+        row_codes = jnp.concatenate([picked_codes_ref[user], codes[:HALO]], axis=0)
+        similar = last_with_last(queries, rows)
+        agreement = last_with_last(query_codes, row_codes)
+        scores = similar * (1.0 / math.sqrt(width)) + HASH_WEIGHT / code_bits * agreement
+        usable = jnp.concatenate([masks_ref[user, 0:1], masks_ref[user, 1:2]], axis=1) > 0.0
         group_max = jnp.max(jnp.where(usable, scores, NEG_FILL), axis=1, keepdims=True)
         weights = jnp.where(usable, jnp.exp(scores - group_max), 0.0)
         group_total = jnp.sum(weights, axis=1, keepdims=True)
-        part_ref[user, :, :feature_width] = jnp.dot(
-            weights.astype(jnp.bfloat16), picked, preferred_element_type=jnp.float32
+        part_ref[user, :, :width] = jnp.dot(
+            weights.astype(jnp.bfloat16), rows, preferred_element_type=jnp.float32
         )
         side_lane = lax.broadcasted_iota(jnp.int32, (queries.shape[0], SIDE), 1)
-        part_ref[user, :, feature_width:] = jnp.where(
-            side_lane < SIDE // 2, group_max, group_total
-        )
+        part_ref[user, :, width:] = jnp.where(side_lane < SIDE // 2, group_max, group_total)
 
 
 def merge_kernel(mine_ref, other_ref, own_ref, moments_ref):
@@ -214,52 +237,57 @@
     f32, bf16 = jnp.float32, jnp.bfloat16
     in_vmem = pl.BlockSpec(memory_space=pltpu.VMEM)
     swap = [(0, 1), (1, 0)]
-    other = lax.ppermute(
-        jnp.concatenate([behaviors[:, group_rows - HALO :], candidates], axis=1), "seq", swap
-    )
-    loads = users * group_rows // CHUNK
-    picked, live, gain, bias = pl.pallas_call(
+    bits = hash_planes.shape[1]
+    arguments = (ranks, lengths, norm_gain, norm_bias, hash_planes.T, candidates, behaviors)
+    params = pltpu.CompilerParams(vmem_limit_bytes=VMEM_LIMIT)
+    sent, rows, mine, places, gain, bias, planes = pl.pallas_call(
+        load_kernel,
+        out_shape=(
+            jax.ShapeDtypeStruct((users, HALO + own_cands, width), bf16),
+            jax.ShapeDtypeStruct(behaviors.shape, bf16),
+            jax.ShapeDtypeStruct(candidates.shape, bf16),
+            jax.ShapeDtypeStruct(ranks.shape, jnp.int32),
+            jax.ShapeDtypeStruct(norm_gain.shape, f32),
+            jax.ShapeDtypeStruct(norm_bias.shape, f32),
+            jax.ShapeDtypeStruct((bits, width), bf16),
+        ),
+        in_specs=[pl.BlockSpec(memory_space=pl.ANY)] * len(arguments),
+        out_specs=(in_vmem,) * 7,
+        scratch_shapes=[
+            pltpu.VMEM(ranks.shape, jnp.int32),
+            pltpu.SMEM(lengths.shape, jnp.int32),
+            pltpu.SemaphoreType.DMA((7 + users * (HALO // TAIL_CHUNK + group_rows // CHUNK),)),
+        ],
+        compiler_params=params,
+        name="load",
+    )(*(pltpu.with_memory_space_constraint(value, pltpu.HBM) for value in arguments))
+    other = lax.ppermute(sent, "seq", swap)
+    picked, picked_codes, mine_codes, masks = pl.pallas_call(
         own_picks_kernel,
         out_shape=(
             jax.ShapeDtypeStruct((users, picks, width), bf16),
-            jax.ShapeDtypeStruct((users, 1, picks), f32),
-            jax.ShapeDtypeStruct(norm_gain.shape, f32),
-            jax.ShapeDtypeStruct(norm_bias.shape, f32),
+            jax.ShapeDtypeStruct((users, picks, bits), bf16),
+            jax.ShapeDtypeStruct((users, own_cands, bits), bf16),
+            jax.ShapeDtypeStruct((users, 2, picks), f32),
         ),
-        in_specs=[
-            in_vmem,
-            pl.BlockSpec(memory_space=pltpu.SMEM),
-            in_vmem,
-            in_vmem,
-            pl.BlockSpec(memory_space=pl.ANY),
-        ],
+        in_specs=[in_vmem] * 4,
         out_specs=(in_vmem,) * 4,
-        scratch_shapes=[
-            pltpu.VMEM(behaviors.shape, bf16),
-            pltpu.SemaphoreType.DMA((loads,)),
-        ],
         cost_estimate=pl.CostEstimate(
             flops=2 * users * picks * group_rows * width,
             bytes_accessed=behaviors.nbytes,
             transcendentals=0,
         ),
-        compiler_params=pltpu.CompilerParams(vmem_limit_bytes=VMEM_LIMIT),
+        compiler_params=params,
         name="own_picks",
-    )(
-        ranks,
-        lengths,
-        norm_gain,
-        norm_bias,
-        pltpu.with_memory_space_constraint(behaviors, pltpu.HBM),
-    )
+    )(places, rows, mine, planes)
     part = pl.pallas_call(
         attend_kernel,
         out_shape=jax.ShapeDtypeStruct((users, cands, width + SIDE), f32),
-        in_specs=[in_vmem] * 6,
+        in_specs=[in_vmem] * 7,
         out_specs=in_vmem,
-        compiler_params=pltpu.CompilerParams(vmem_limit_bytes=VMEM_LIMIT),
+        compiler_params=params,
         name="attend",
-    )(ranks, live, picked, candidates, other, hash_planes.T)
+    )(masks, picked, picked_codes, mine, mine_codes, other, planes)
     own, moments = pl.pallas_call(
         merge_kernel,
         out_shape=(
@@ -268,7 +296,7 @@
         ),
         in_specs=[in_vmem] * 2,
         out_specs=(in_vmem,) * 2,
-        compiler_params=pltpu.CompilerParams(vmem_limit_bytes=VMEM_LIMIT),
+        compiler_params=params,
         name="merge",
     )(part, lax.ppermute(part, "seq", swap))
     row_count = users * cands * lax.axis_size("user")

time: 22 us -> 20.5 us (0.932)
  local copies, waits for them, and re-layouts: 1.02 us -> 0 us
  Pallas kernels: 3.71 us -> 3.23 us
  waiting for transfers between devices: 6.31 us -> 6.54 us
    pallas_call x1, Pallas kernels: 2.3 us -> 0.8 us  [two_groups(): pl.pallas_call(own_picks_kernel, out_shape=(jax.ShapeDtypeStruct((users,...]
    pallas_call x0 -> x1, Pallas kernels: none -> 1.46 us  [two_groups(): pl.pallas_call(load_kernel, out_shape=(jax.ShapeDtypeStruct((users, HALO...]
    slice x2 -> x0, local copies, waits for them, and re-layouts: 0.9 us -> none  [two_groups(): behaviors[:, group_rows - HALO:]]
    pallas_call x1, Pallas kernels: 1.19 us -> 0.75 us  [two_groups(): pl.pallas_call(attend_kernel, out_shape=jax.ShapeDtypeStruct((users, cand...]
    ppermute x1, waiting for transfers between devices: 0.01 us -> 0.23 us  [two_groups(): other = lax.ppermute(sent, 'seq', swap)]
  transfers between devices with their start and end apart: 6 -> 6, of which waited for: 5 -> 6; matrix products, arithmetic and copies ran while one was open for 0% -> 0% of each run, Pallas kernels for 11% -> 4%
where the time goes in v3:
time: 20.5 us; the launch traced here: 20.3 us
  starting transfers between devices  9.85 us (48%)
  waiting for transfers between devices  6.54 us (32%)
  Pallas kernels  3.23 us (16%)
  other arithmetic  0.66 us (3%)
    ppermute x4, starting transfers between devices, user_total(): value = value + lax.ppermute(value, BOTH, pairs)  8.86 us
    ppermute x4, waiting for transfers between devices, user_total(): value = value + lax.ppermute(value, BOTH, pairs)  5.24 us
    pallas_call x1, Pallas kernels, two_groups(): pl.pallas_call(load_kernel, out_shape=(jax.ShapeDtypeStruct((users, HALO...  1.46 us
    ppermute x1, waiting for transfers between devices, two_groups(): lax.ppermute(part, 'seq', swap)  1.07 us
    pallas_call x1, Pallas kernels, two_groups(): pl.pallas_call(own_picks_kernel, out_shape=(jax.ShapeDtypeStruct((users,...  0.8 us
    pallas_call x1, Pallas kernels, two_groups(): pl.pallas_call(attend_kernel, out_shape=jax.ShapeDtypeStruct((users, cand...  0.75 us
    convert_element_type x1, other arithmetic, normalized(): return normed.astype(jnp.bfloat16)  0.63 us
    ppermute x1, starting transfers between devices, two_groups(): other = lax.ppermute(sent, 'seq', swap)  0.56 us
  transfers between devices with their start and end apart: 6, of which 6 were waited for; matrix products, arithmetic and copies ran while one was open for 0% of the time, Pallas kernels for 4%

profile of v3, /device:TPU:0, one launch (start us, length us, event | category | flops | bytes accessed | tf_op | source)
XLA Modules:
  0.0 20.3 jit_solution(17093696765387847925)
XLA Ops:
  0.0 1.5 %load.1 = (bf16[2,160,256]{2,1,0:T(8,128)(2,1)S(1)}, bf16[2,1024,256]{2,1,0:T(8,128)(2,1)S(1)}, bf16[2,32,256]{2,1,0:T(8,128)(2,1)S(1)}, s32[2,1,128]{2,1,0:T(1,...) custom-call(s32[2,1,128]{2,1,0:T(1,128)} %ranks_hbm.1, s32[2]{0:T(128)} %lengths_hbm.1, ...), custom_call_target="tpu_custom_call" | custom-call | tf_op jit(solution)/shard_map/load/pallas_call | solution.py:243
  1.5 0.6 %collective-permute-start = (bf16[2,160,256]{2,1,0:T(8,128)(2,1)S(1)}, bf16[2,160,256]{2,1,0:T(8,128)(2,1)S(1)}, u32[]{:S(2)}, u32[]{:S(2)}) collective-permute-start(bf16[2,160,256]{2,1,0:T(8,128)(2,1)S(1)} %get-tuple-element.26), channel_id=1, source_target_pairs={{0,1},{1,0},{2,3},{3,2},{4,5},{5,4},{6,7},{7,6},{8,9},{9,8},{10,11... | collective-permute-start | bytes 491528 | tf_op jit(solution)/shard_map/ppermute | solution.py:264
  2.0 0.8 %own_picks.1 = (bf16[2,128,256]{2,1,0:T(8,128)(2,1)S(1)}, bf16[2,128,64]{2,1,0:T(8,128)(2,1)S(1)}, bf16[2,32,64]{2,1,0:T(8,128)(2,1)S(1)}, f32[2,2,128]{2,1,0:T(2,128)S(1)}) custom-call(s32[2,1,128]{2,1,0:T(1,128)S(1)} %get-tuple-element.18.places_ref, bf16[2,1024,256]{2,1,0:T(8,128)(2,1)S(1)} %get-tuple-element.19.rows_ref, ...), custom_call_target="tpu_custom_call" | custom-call | flops 134217728 | bytes 1048576 | tf_op jit(solution)/shard_map/own_picks/pallas_call | solution.py:265
  2.8 0.2 %collective-permute-done.other_ref = bf16[2,160,256]{2,1,0:T(8,128)(2,1)S(1)} collective-permute-done((bf16[2,160,256]{2,1,0:T(8,128)(2,1)S(1)}, bf16[2,160,256]{2,1,0:T(8,128)(2,1)S(1)}, u32[]{:S(2)}, u32[]{:S(2)}) %collective-permute-start) | collective-permute-done | bytes 163872 | tf_op jit(solution)/shard_map/ppermute | solution.py:264
  3.1 0.7 %attend.1.mine_ref = f32[2,64,384]{2,1,0:T(8,128)S(1)} custom-call(f32[2,2,128]{2,1,0:T(2,128)S(1)} %get-tuple-element.22.masks_ref, bf16[2,128,256]{2,1,0:T(8,128)(2,1)S(1)} %get-tuple-element.23.picked_ref, bf16[2,128,64]{2,1,0:T(8,128)(2,1)S(1)} %get-tuple-element.24.picked_codes_ref, bf16[2,32,256]{2,1,0:T(8,128)(2,1)S(1)} %get-tuple-element.20.mine_ref, ...), custom_call_target="tpu_custom_call" | custom-call | tf_op jit(solution)/shard_map/attend/pallas_call | solution.py:283
  3.8 0.4 %collective-permute-start.1 = (f32[2,64,384]{2,1,0:T(8,128)S(1)}, f32[2,64,384]{2,1,0:T(8,128)S(1)}, u32[]{:S(2)}, u32[]{:S(2)}) collective-permute-start(f32[2,64,384]{2,1,0:T(8,128)S(1)} %attend.1.mine_ref), channel_id=1, source_target_pairs={{0,1},{1,0},{2,3},{3,2},{4,5},{5,4},{6,7},{7,6},{8,9},{9,8},{10,11... | collective-permute-start | bytes 589832 | tf_op jit(solution)/shard_map/ppermute | solution.py:301
  4.2 1.1 %collective-permute-done.1.other_ref = f32[2,64,384]{2,1,0:T(8,128)S(1)} collective-permute-done((f32[2,64,384]{2,1,0:T(8,128)S(1)}, f32[2,64,384]{2,1,0:T(8,128)S(1)}, u32[]{:S(2)}, u32[]{:S(2)}) %collective-permute-start.1) | collective-permute-done | bytes 196640 | tf_op jit(solution)/shard_map/ppermute | solution.py:301
  5.3 0.2 %merge.1 = (f32[2,32,256]{2,1,0:T(8,128)S(1)}, f32[2,256]{1,0:T(2,128)S(1)}) custom-call(f32[2,64,384]{2,1,0:T(8,128)S(1)} %attend.1.mine_ref, f32[2,64,384]{2,1,0:T(8,128)S(1)} %collective-permute-done.1.other_ref), custom_call_target="tpu_custom_call" | custom-call | tf_op jit(solution)/shard_map/merge/pallas_call | solution.py:291
  5.5 2.7 %collective-permute-start.2 = (f32[2,256]{1,0:T(2,128)S(1)}, f32[2,256]{1,0:T(2,128)S(1)}, u32[]{:S(2)}, u32[]{:S(2)}) collective-permute-start(f32[2,256]{1,0:T(2,128)S(1)} %get-tuple-element.28), channel_id=1, source_target_pairs={{0,3},{1,2},{2,1},{3,0},{4,7},{5,6},{6,5},{7,4},{8,11},{9,10},{10,... | collective-permute-start | bytes 6152 | tf_op jit(solution)/shard_map/ppermute | solution.py:35
  8.2 1.3 %collective-permute-done.2 = f32[2,256]{1,0:T(2,128)S(1)} collective-permute-done((f32[2,256]{1,0:T(2,128)S(1)}, f32[2,256]{1,0:T(2,128)S(1)}, u32[]{:S(2)}, u32[]{:S(2)}) %collective-permute-start.2) | collective-permute-done | bytes 2080 | tf_op jit(solution)/shard_map/ppermute | solution.py:35
  9.5 1.7 %collective-permute-start.3 = (f32[2,256]{1,0:T(2,128)S(1)}, f32[2,256]{1,0:T(2,128)S(1)}, u32[]{:S(2)}, u32[]{:S(2)}) collective-permute-start(f32[2,256]{1,0:T(2,128)S(1)} %add.30), channel_id=1, source_target_pairs={{0,5},{1,4},{2,7},{3,6},{4,1},{5,0},{6,3},{7,2},{8,13},{9,12},{10,... | collective-permute-start | bytes 6152 | tf_op jit(solution)/shard_map/ppermute | solution.py:35
  11.2 1.3 %collective-permute-done.3 = f32[2,256]{1,0:T(2,128)S(1)} collective-permute-done((f32[2,256]{1,0:T(2,128)S(1)}, f32[2,256]{1,0:T(2,128)S(1)}, u32[]{:S(2)}, u32[]{:S(2)}) %collective-permute-start.3) | collective-permute-done | bytes 2080 | tf_op jit(solution)/shard_map/ppermute | solution.py:35
  12.6 1.8 %collective-permute-start.4 = (f32[2,256]{1,0:T(2,128)S(1)}, f32[2,256]{1,0:T(2,128)S(1)}, u32[]{:S(2)}, u32[]{:S(2)}) collective-permute-start(f32[2,256]{1,0:T(2,128)S(1)} %add.31), channel_id=1, source_target_pairs={{0,9},{1,8},{2,11},{3,10},{4,13},{5,12},{6,15},{7,14},{8,1},{9,0},... | collective-permute-start | bytes 6152 | tf_op jit(solution)/shard_map/ppermute | solution.py:35
  14.3 1.3 %collective-permute-done.4 = f32[2,256]{1,0:T(2,128)S(1)} collective-permute-done((f32[2,256]{1,0:T(2,128)S(1)}, f32[2,256]{1,0:T(2,128)S(1)}, u32[]{:S(2)}, u32[]{:S(2)}) %collective-permute-start.4) | collective-permute-done | bytes 2080 | tf_op jit(solution)/shard_map/ppermute | solution.py:35
  15.6 2.7 %collective-permute-start.5 = (f32[2,256]{1,0:T(2,128)S(1)}, f32[2,256]{1,0:T(2,128)S(1)}, u32[]{:S(2)}, u32[]{:S(2)}) collective-permute-start(f32[2,256]{1,0:T(2,128)S(1)} %add.32), channel_id=1, source_target_pairs={{0,17},{1,16},{2,19},{3,18},{4,21},{5,20},{6,23},{7,22},{8,25},{9,... | collective-permute-start | bytes 6152 | tf_op jit(solution)/shard_map/ppermute | solution.py:35
  18.3 1.3 %collective-permute-done.5 = f32[2,256]{1,0:T(2,128)S(1)} collective-permute-done((f32[2,256]{1,0:T(2,128)S(1)}, f32[2,256]{1,0:T(2,128)S(1)}, u32[]{:S(2)}, u32[]{:S(2)}) %collective-permute-start.5) | collective-permute-done | bytes 2080 | tf_op jit(solution)/shard_map/ppermute | solution.py:35
  19.7 0.6 %add_convert_fusion = bf16[2,32,256]{2,1,0:T(8,128)(2,1)} fusion(f32[2,32,256]{2,1,0:T(8,128)S(1)} %get-tuple-element.27, f32[256]{0:T(256)S(1)} %get-tuple-element.30, f32[256]{0:T(256)S(1)} %get-tuple-element.29, f32[256]{0:T(256)S(1)} %add_rsqrt_fusion, f32[256]{0:T(256)S(1)} %bitcast.5), kind=kLoop, calls=%fused_computation | loop fusion | flops 81920 | bytes 102400 | tf_op jit(solution)/shard_map/convert_element_type | solution.py:54
  (6 shorter events, 0.0 us)
Async XLA Ops:
  1.5 1.6 %collective-permute-start = (bf16[2,160,256]{2,1,0:T(8,128)(2,1)S(1)}, bf16[2,160,256]{2,1,0:T(8,128)(2,1)S(1)}, u32[]{:S(2)}, u32[]{:S(2)}) collective-permute-start(bf16[2,160,256]{2,1,0:T(8,128)(2,1)S(1)} %get-tuple-element.26), channel_id=1, source_target_pairs={{0,1},{1,0},{2,3},{3,2},{4,5},{5,4},{6,7},{7,6},{8,9},{9,8},{10,11... | collective-permute-start | bytes 491528 | tf_op jit(solution)/shard_map/ppermute | solution.py:264
  3.8 1.5 %collective-permute-start.1 = (f32[2,64,384]{2,1,0:T(8,128)S(1)}, f32[2,64,384]{2,1,0:T(8,128)S(1)}, u32[]{:S(2)}, u32[]{:S(2)}) collective-permute-start(f32[2,64,384]{2,1,0:T(8,128)S(1)} %attend.1.mine_ref), channel_id=1, source_target_pairs={{0,1},{1,0},{2,3},{3,2},{4,5},{5,4},{6,7},{7,6},{8,9},{9,8},{10,11... | collective-permute-start | bytes 589832 | tf_op jit(solution)/shard_map/ppermute | solution.py:301
  5.5 4.0 %collective-permute-start.2 = (f32[2,256]{1,0:T(2,128)S(1)}, f32[2,256]{1,0:T(2,128)S(1)}, u32[]{:S(2)}, u32[]{:S(2)}) collective-permute-start(f32[2,256]{1,0:T(2,128)S(1)} %get-tuple-element.28), channel_id=1, source_target_pairs={{0,3},{1,2},{2,1},{3,0},{4,7},{5,6},{6,5},{7,4},{8,11},{9,10},{10,... | collective-permute-start | bytes 6152 | tf_op jit(solution)/shard_map/ppermute | solution.py:35
  9.5 3.0 %collective-permute-start.3 = (f32[2,256]{1,0:T(2,128)S(1)}, f32[2,256]{1,0:T(2,128)S(1)}, u32[]{:S(2)}, u32[]{:S(2)}) collective-permute-start(f32[2,256]{1,0:T(2,128)S(1)} %add.30), channel_id=1, source_target_pairs={{0,5},{1,4},{2,7},{3,6},{4,1},{5,0},{6,3},{7,2},{8,13},{9,12},{10,... | collective-permute-start | bytes 6152 | tf_op jit(solution)/shard_map/ppermute | solution.py:35
  12.6 3.1 %collective-permute-start.4 = (f32[2,256]{1,0:T(2,128)S(1)}, f32[2,256]{1,0:T(2,128)S(1)}, u32[]{:S(2)}, u32[]{:S(2)}) collective-permute-start(f32[2,256]{1,0:T(2,128)S(1)} %add.31), channel_id=1, source_target_pairs={{0,9},{1,8},{2,11},{3,10},{4,13},{5,12},{6,15},{7,14},{8,1},{9,0},... | collective-permute-start | bytes 6152 | tf_op jit(solution)/shard_map/ppermute | solution.py:35
  15.6 4.0 %collective-permute-start.5 = (f32[2,256]{1,0:T(2,128)S(1)}, f32[2,256]{1,0:T(2,128)S(1)}, u32[]{:S(2)}, u32[]{:S(2)}) collective-permute-start(f32[2,256]{1,0:T(2,128)S(1)} %add.32), channel_id=1, source_target_pairs={{0,17},{1,16},{2,19},{3,18},{4,21},{5,20},{6,23},{7,22},{8,25},{9,... | collective-permute-start | bytes 6152 | tf_op jit(solution)/shard_map/ppermute | solution.py:35

commit v4 on v3

--- a/solution.py
+++ b/solution.py
@@ -16,9 +16,8 @@
 
 BOTH = ("user", "seq")
 SIDE = 128
-CHUNK = 1024
-TAIL_CHUNK = 128
 VMEM_LIMIT = 8 * 1024 * 1024
+LOAD_COST = 10**8
 
 
 def user_total(value):
@@ -107,7 +106,7 @@
 
 def load_kernel(
     ranks_hbm, lengths_hbm, norm_gain_hbm, norm_bias_hbm, planes_hbm, mine_hbm, behaviors_hbm,
-    sent_ref, rows_ref, mine_ref, places_ref, gain_ref, bias_ref, planes_ref,
+    sent_ref, places_ref, gain_ref, bias_ref, planes_ref,
     ranks, lengths, sems,
 ):
     users, group_rows, _ = behaviors_hbm.shape
@@ -115,24 +114,12 @@
     pairs = [
         (ranks_hbm, ranks),
         (lengths_hbm, lengths),
+        (mine_hbm, sent_ref.at[:, pl.ds(HALO, mine_hbm.shape[1])]),
+        (behaviors_hbm.at[:, pl.ds(tail, HALO)], sent_ref.at[:, pl.ds(0, HALO)]),
         (planes_hbm, planes_ref),
-        (mine_hbm, mine_ref),
-        (mine_hbm, sent_ref.at[:, pl.ds(HALO, mine_ref.shape[1])]),
         (norm_gain_hbm, gain_ref),
         (norm_bias_hbm, bias_ref),
     ]
-    for user in range(users):
-        for first in range(0, HALO, TAIL_CHUNK):
-            pairs.append(
-                (
-                    behaviors_hbm.at[user, pl.ds(tail + first, TAIL_CHUNK)],
-                    sent_ref.at[user, pl.ds(first, TAIL_CHUNK)],
-                )
-            )
-    for user in range(users):
-        for first in range(0, group_rows, CHUNK):
-            part = (user, pl.ds(first, CHUNK))
-            pairs.append((behaviors_hbm.at[part], rows_ref.at[part]))
     copies = [
         pltpu.make_async_copy(source, target, sems.at[k])
         for k, (source, target) in enumerate(pairs)
@@ -151,7 +138,7 @@
 
 
 def own_picks_kernel(
-    places_ref, rows_ref, mine_ref, planes_ref,
+    places_ref, rows_ref, sent_ref, planes_ref,
     picked_ref, picked_codes_ref, mine_codes_ref, masks_ref,
 ):
     users, group_rows, _ = rows_ref.shape
@@ -171,62 +158,86 @@
         )
         picked_ref[user] = picked
         picked_codes_ref[user] = soft_codes(picked, planes)
-        mine_codes_ref[user] = soft_codes(mine_ref[user], planes)
+        mine_codes_ref[user] = soft_codes(sent_ref[user, HALO:], planes)
 
 
 def attend_kernel(
-    masks_ref, picked_ref, picked_codes_ref, mine_ref, mine_codes_ref, other_ref, planes_ref,
+    masks_ref, picked_ref, picked_codes_ref, sent_ref, mine_codes_ref, other_ref, planes_ref,
     part_ref,
 ):
-    users, _, width = picked_ref.shape
+    user_count, _, width = picked_ref.shape
+    users = range(user_count)
     code_bits = planes_ref.shape[0]
     planes = planes_ref[...]
-    for user in range(users):
-        codes = soft_codes(other_ref[user], planes)
-        queries = jnp.concatenate([mine_ref[user], other_ref[user, HALO:]], axis=0)
-        query_codes = jnp.concatenate([mine_codes_ref[user], codes[HALO:]], axis=0)
-        rows = jnp.concatenate([picked_ref[user], other_ref[user, :HALO]], axis=0)
-        row_codes = jnp.concatenate([picked_codes_ref[user], codes[:HALO]], axis=0)
-        similar = last_with_last(queries, rows)
+    codes = [soft_codes(other_ref[user], planes) for user in users]
+    rows, similar = [], []
+    for user in users:
+        queries = jnp.concatenate([sent_ref[user, HALO:], other_ref[user, HALO:]], axis=0)
+        rows.append(jnp.concatenate([picked_ref[user], other_ref[user, :HALO]], axis=0))
+        similar.append(last_with_last(queries, rows[user]) * (1.0 / math.sqrt(width)))
+    scores, usable = [], []
+    for user in users:
+        query_codes = jnp.concatenate([mine_codes_ref[user], codes[user][HALO:]], axis=0)
+        row_codes = jnp.concatenate([picked_codes_ref[user], codes[user][:HALO]], axis=0)
         agreement = last_with_last(query_codes, row_codes)
-        scores = similar * (1.0 / math.sqrt(width)) + HASH_WEIGHT / code_bits * agreement
-        usable = jnp.concatenate([masks_ref[user, 0:1], masks_ref[user, 1:2]], axis=1) > 0.0
-        group_max = jnp.max(jnp.where(usable, scores, NEG_FILL), axis=1, keepdims=True)
-        weights = jnp.where(usable, jnp.exp(scores - group_max), 0.0)
-        group_total = jnp.sum(weights, axis=1, keepdims=True)
+        scores.append(similar[user] + HASH_WEIGHT / code_bits * agreement)
+        usable.append(
+            jnp.concatenate([masks_ref[user, 0:1], masks_ref[user, 1:2]], axis=1) > 0.0
+        )
+    group_max = [
+        jnp.max(jnp.where(usable[user], scores[user], NEG_FILL), axis=1, keepdims=True)
+        for user in users
+    ]
+    weights = [
+        jnp.where(usable[user], jnp.exp(scores[user] - group_max[user]), 0.0) for user in users
+    ]
+    for user in users:
         part_ref[user, :, :width] = jnp.dot(
-            weights.astype(jnp.bfloat16), rows, preferred_element_type=jnp.float32
+            weights[user].astype(jnp.bfloat16), rows[user], preferred_element_type=jnp.float32
         )
-        side_lane = lax.broadcasted_iota(jnp.int32, (queries.shape[0], SIDE), 1)
-        part_ref[user, :, width:] = jnp.where(side_lane < SIDE // 2, group_max, group_total)
+    for user in users:
+        group_total = jnp.sum(weights[user], axis=1, keepdims=True)
+        side_lane = lax.broadcasted_iota(jnp.int32, (group_total.shape[0], SIDE), 1)
+        part_ref[user, :, width:] = jnp.where(
+            side_lane < SIDE // 2, group_max[user], group_total
+        )
 
 
 def merge_kernel(mine_ref, other_ref, own_ref, moments_ref):
     users, cands, packed = mine_ref.shape
     width = packed - SIDE
     half = cands // 2
-    sums = jnp.zeros((1, width), jnp.float32)
-    squares = jnp.zeros((1, width), jnp.float32)
+    low = lax.broadcasted_iota(jnp.int32, (half, SIDE), 1) < SIDE // 2
+    sums, squares = [], []
     for user in range(users):
         for first in (0, half):
-            left = mine_ref[user, first : first + half]
-            right = other_ref[user, half - first : cands - first]
-            left_top, right_top = left[:, width : width + 1], right[:, width : width + 1]
-            last = width + SIDE // 2
-            joint_max = jnp.maximum(left_top, right_top)
-            left_scale = jnp.exp(left_top - joint_max)
-            right_scale = jnp.exp(right_top - joint_max)
-            numerator = left_scale * left[:, :width] + right_scale * right[:, :width]
-            denominator = (
-                left_scale * left[:, last : last + 1] + right_scale * right[:, last : last + 1]
+            here = (user, slice(first, first + half))
+            there = (user, slice(half - first, cands - first))
+            tops, totals = [], []
+            for ref, at in ((mine_ref, here), (other_ref, there)):
+                side = ref[at[0], at[1], width:]
+                turned = pltpu.roll(side, SIDE // 2, 1)
+                tops.append(jnp.where(low, side, turned))
+                totals.append(jnp.where(low, turned, side))
+            joint_max = jnp.maximum(*tops)
+            scales = [jnp.exp(top - joint_max) for top in tops]
+            denominator = scales[0] * totals[0] + scales[1] * totals[1]
+            for column in range(0, width, SIDE):
+                lanes = slice(column, column + SIDE)
+                numerator = (
+                    scales[0] * mine_ref[here[0], here[1], lanes]
+                    + scales[1] * other_ref[there[0], there[1], lanes]
+                )
+                attended = numerator / denominator
+                sums.append((column, jnp.sum(attended, axis=0, keepdims=True)))
+                squares.append((column, jnp.sum(attended * attended, axis=0, keepdims=True)))
+                if first == 0:
+                    own_ref[user, :, lanes] = attended
+    for row, terms in enumerate((sums, squares)):
+        for column in range(0, width, SIDE):
+            moments_ref[row : row + 1, column : column + SIDE] = sum(
+                term for at, term in terms if at == column
             )
-            attended = numerator / denominator
-            sums += jnp.sum(attended, axis=0, keepdims=True)
-            squares += jnp.sum(attended * attended, axis=0, keepdims=True)
-            if first == 0:
-                own_ref[user] = attended
-    moments_ref[0:1] = sums
-    moments_ref[1:2] = squares
 
 
 def two_groups(behaviors, candidates, ranks, lengths, hash_planes, norm_gain, norm_bias):
@@ -240,24 +251,24 @@
     bits = hash_planes.shape[1]
     arguments = (ranks, lengths, norm_gain, norm_bias, hash_planes.T, candidates, behaviors)
     params = pltpu.CompilerParams(vmem_limit_bytes=VMEM_LIMIT)
-    sent, rows, mine, places, gain, bias, planes = pl.pallas_call(
+    sent_bytes = 2 * users * (HALO + own_cands) * width
+    sent, places, gain, bias, planes = pl.pallas_call(
         load_kernel,
         out_shape=(
             jax.ShapeDtypeStruct((users, HALO + own_cands, width), bf16),
-            jax.ShapeDtypeStruct(behaviors.shape, bf16),
-            jax.ShapeDtypeStruct(candidates.shape, bf16),
             jax.ShapeDtypeStruct(ranks.shape, jnp.int32),
             jax.ShapeDtypeStruct(norm_gain.shape, f32),
             jax.ShapeDtypeStruct(norm_bias.shape, f32),
             jax.ShapeDtypeStruct((bits, width), bf16),
         ),
         in_specs=[pl.BlockSpec(memory_space=pl.ANY)] * len(arguments),
-        out_specs=(in_vmem,) * 7,
+        out_specs=(in_vmem,) * 5,
         scratch_shapes=[
             pltpu.VMEM(ranks.shape, jnp.int32),
             pltpu.SMEM(lengths.shape, jnp.int32),
-            pltpu.SemaphoreType.DMA((7 + users * (HALO // TAIL_CHUNK + group_rows // CHUNK),)),
+            pltpu.SemaphoreType.DMA((len(arguments),)),
         ],
+        cost_estimate=pl.CostEstimate(flops=LOAD_COST, bytes_accessed=sent_bytes, transcendentals=0),
         compiler_params=params,
         name="load",
     )(*(pltpu.with_memory_space_constraint(value, pltpu.HBM) for value in arguments))
@@ -279,7 +290,7 @@
         ),
         compiler_params=params,
         name="own_picks",
-    )(places, rows, mine, planes)
+    )(places, behaviors, sent, planes)
     part = pl.pallas_call(
         attend_kernel,
         out_shape=jax.ShapeDtypeStruct((users, cands, width + SIDE), f32),
@@ -287,7 +298,7 @@
         out_specs=in_vmem,
         compiler_params=params,
         name="attend",
-    )(masks, picked, picked_codes, mine, mine_codes, other, planes)
+    )(masks, picked, picked_codes, sent, mine_codes, other, planes)
     own, moments = pl.pallas_call(
         merge_kernel,
         out_shape=(

time: 20.5 us -> 19.8 us (0.966)
  Pallas kernels: 3.23 us -> 2.59 us
    pallas_call x1, Pallas kernels: 1.46 us -> 1.09 us  [two_groups(): pl.pallas_call(load_kernel, out_shape=(jax.ShapeDtypeStruct((users, HALO...]
where the time goes in v4:
time: 19.8 us; the launch traced here: 19.7 us
  starting transfers between devices  9.85 us (50%)
  waiting for transfers between devices  6.53 us (33%)
  Pallas kernels  2.59 us (13%)
  other arithmetic  0.66 us (3%)
    ppermute x4, starting transfers between devices, user_total(): value = value + lax.ppermute(value, BOTH, pairs)  8.86 us
    ppermute x4, waiting for transfers between devices, user_total(): value = value + lax.ppermute(value, BOTH, pairs)  5.24 us
    pallas_call x1, Pallas kernels, two_groups(): pl.pallas_call(load_kernel, out_shape=(jax.ShapeDtypeStruct((users, HALO...  1.09 us
    ppermute x1, waiting for transfers between devices, two_groups(): lax.ppermute(part, 'seq', swap)  1.07 us
    pallas_call x1, Pallas kernels, two_groups(): pl.pallas_call(own_picks_kernel, out_shape=(jax.ShapeDtypeStruct((users,...  0.8 us
    convert_element_type x1, other arithmetic, normalized(): return normed.astype(jnp.bfloat16)  0.63 us
    ppermute x1, starting transfers between devices, two_groups(): other = lax.ppermute(sent, 'seq', swap)  0.56 us
    pallas_call x1, Pallas kernels, two_groups(): pl.pallas_call(attend_kernel, out_shape=jax.ShapeDtypeStruct((users, cand...  0.55 us
  transfers between devices with their start and end apart: 6, of which 6 were waited for; matrix products, arithmetic and copies ran while one was open for 0% of the time, Pallas kernels for 4%

profile of v4, /device:TPU:0, one launch (start us, length us, event | category | flops | bytes accessed | tf_op | source)
XLA Modules:
  0.0 19.7 jit_solution(12134707586636725971)
XLA Ops:
  0.0 0.0 copy-start
  0.0 1.1 %load.1 = (bf16[2,160,256]{2,1,0:T(8,128)(2,1)S(1)}, s32[2,1,128]{2,1,0:T(1,128)S(1)}, f32[256]{0:T(256)S(1)}, f32[256]{0:T(256)S(1)}, bf16[64,256]{1,0:T(8,128)(2,1)S(1)}) custom-call(s32[2,1,128]{2,1,0:T(1,128)} %ranks_hbm.1, s32[2]{0:T(128)} %lengths_hbm.1, f32[256]{0:T(256)} %norm_gain_hbm.1, f32[256]{0:T(256)} %norm_bias_hbm.1, ...), custom_call_target="tpu_custom_call" | custom-call | flops 100000000 | bytes 163840 | tf_op jit(solution)/shard_map/load/pallas_call | solution.py:255
  1.1 0.6 %collective-permute-start = (bf16[2,160,256]{2,1,0:T(8,128)(2,1)S(1)}, bf16[2,160,256]{2,1,0:T(8,128)(2,1)S(1)}, u32[]{:S(2)}, u32[]{:S(2)}) collective-permute-start(bf16[2,160,256]{2,1,0:T(8,128)(2,1)S(1)} %get-tuple-element.17.sent_ref), channel_id=1, source_target_pairs={{0,1},{1,0},{2,3},{3,2},{4,5},{5,4},{6,7},{7,6},{8,9},{9,8},{10,11... | collective-permute-start | bytes 491528 | tf_op jit(solution)/shard_map/ppermute | solution.py:275
  1.7 0.0 copy-done
  1.7 0.8 %own_picks.1 = (bf16[2,128,256]{2,1,0:T(8,128)(2,1)S(1)}, bf16[2,128,64]{2,1,0:T(8,128)(2,1)S(1)}, bf16[2,32,64]{2,1,0:T(8,128)(2,1)S(1)}, f32[2,2,128]{2,1,0:T(2,128)S(1)}) custom-call(s32[2,1,128]{2,1,0:T(1,128)S(1)} %get-tuple-element.16.places_ref, bf16[2,1024,256]{2,1,0:T(8,128)(2,1)S(1)} %copy-done, ...), custom_call_target="tpu_custom_call" | custom-call | flops 134217728 | bytes 1048576 | tf_op jit(solution)/shard_map/own_picks/pallas_call | solution.py:276
  2.5 0.2 %collective-permute-done.other_ref = bf16[2,160,256]{2,1,0:T(8,128)(2,1)S(1)} collective-permute-done((bf16[2,160,256]{2,1,0:T(8,128)(2,1)S(1)}, bf16[2,160,256]{2,1,0:T(8,128)(2,1)S(1)}, u32[]{:S(2)}, u32[]{:S(2)}) %collective-permute-start) | collective-permute-done | bytes 163872 | tf_op jit(solution)/shard_map/ppermute | solution.py:275
  2.7 0.5 %attend.1.mine_ref = f32[2,64,384]{2,1,0:T(8,128)S(1)} custom-call(f32[2,2,128]{2,1,0:T(2,128)S(1)} %get-tuple-element.19.masks_ref, bf16[2,128,256]{2,1,0:T(8,128)(2,1)S(1)} %get-tuple-element.20.picked_ref, bf16[2,128,64]{2,1,0:T(8,128)(2,1)S(1)} %get-tuple-element.21.picked_codes_ref, bf16[2,160,256]{2,1,0:T(8,128)(2,1)S(1)} %get-tuple-element.17.sent_ref, ...), custom_call_target="tpu_custom_call" | custom-call | tf_op jit(solution)/shard_map/attend/pallas_call | solution.py:294
  3.2 0.4 %collective-permute-start.1 = (f32[2,64,384]{2,1,0:T(8,128)S(1)}, f32[2,64,384]{2,1,0:T(8,128)S(1)}, u32[]{:S(2)}, u32[]{:S(2)}) collective-permute-start(f32[2,64,384]{2,1,0:T(8,128)S(1)} %attend.1.mine_ref), channel_id=1, source_target_pairs={{0,1},{1,0},{2,3},{3,2},{4,5},{5,4},{6,7},{7,6},{8,9},{9,8},{10,11... | collective-permute-start | bytes 589832 | tf_op jit(solution)/shard_map/ppermute | solution.py:312
  3.7 1.1 %collective-permute-done.1.other_ref = f32[2,64,384]{2,1,0:T(8,128)S(1)} collective-permute-done((f32[2,64,384]{2,1,0:T(8,128)S(1)}, f32[2,64,384]{2,1,0:T(8,128)S(1)}, u32[]{:S(2)}, u32[]{:S(2)}) %collective-permute-start.1) | collective-permute-done | bytes 196640 | tf_op jit(solution)/shard_map/ppermute | solution.py:312
  4.7 0.2 merge.1
  4.9 2.7 %collective-permute-start.2 = (f32[2,256]{1,0:T(2,128)S(1)}, f32[2,256]{1,0:T(2,128)S(1)}, u32[]{:S(2)}, u32[]{:S(2)}) collective-permute-start(f32[2,256]{1,0:T(2,128)S(1)} %get-tuple-element.24), channel_id=1, source_target_pairs={{0,3},{1,2},{2,1},{3,0},{4,7},{5,6},{6,5},{7,4},{8,11},{9,10},{10,... | collective-permute-start | bytes 6152 | tf_op jit(solution)/shard_map/ppermute | solution.py:34
  7.6 1.3 %collective-permute-done.2 = f32[2,256]{1,0:T(2,128)S(1)} collective-permute-done((f32[2,256]{1,0:T(2,128)S(1)}, f32[2,256]{1,0:T(2,128)S(1)}, u32[]{:S(2)}, u32[]{:S(2)}) %collective-permute-start.2) | collective-permute-done | bytes 2080 | tf_op jit(solution)/shard_map/ppermute | solution.py:34
  8.9 1.7 %collective-permute-start.3 = (f32[2,256]{1,0:T(2,128)S(1)}, f32[2,256]{1,0:T(2,128)S(1)}, u32[]{:S(2)}, u32[]{:S(2)}) collective-permute-start(f32[2,256]{1,0:T(2,128)S(1)} %add.30), channel_id=1, source_target_pairs={{0,5},{1,4},{2,7},{3,6},{4,1},{5,0},{6,3},{7,2},{8,13},{9,12},{10,... | collective-permute-start | bytes 6152 | tf_op jit(solution)/shard_map/ppermute | solution.py:34
  10.6 1.3 %collective-permute-done.3 = f32[2,256]{1,0:T(2,128)S(1)} collective-permute-done((f32[2,256]{1,0:T(2,128)S(1)}, f32[2,256]{1,0:T(2,128)S(1)}, u32[]{:S(2)}, u32[]{:S(2)}) %collective-permute-start.3) | collective-permute-done | bytes 2080 | tf_op jit(solution)/shard_map/ppermute | solution.py:34
  11.9 1.8 %collective-permute-start.4 = (f32[2,256]{1,0:T(2,128)S(1)}, f32[2,256]{1,0:T(2,128)S(1)}, u32[]{:S(2)}, u32[]{:S(2)}) collective-permute-start(f32[2,256]{1,0:T(2,128)S(1)} %add.31), channel_id=1, source_target_pairs={{0,9},{1,8},{2,11},{3,10},{4,13},{5,12},{6,15},{7,14},{8,1},{9,0},... | collective-permute-start | bytes 6152 | tf_op jit(solution)/shard_map/ppermute | solution.py:34
  13.7 1.3 %collective-permute-done.4 = f32[2,256]{1,0:T(2,128)S(1)} collective-permute-done((f32[2,256]{1,0:T(2,128)S(1)}, f32[2,256]{1,0:T(2,128)S(1)}, u32[]{:S(2)}, u32[]{:S(2)}) %collective-permute-start.4) | collective-permute-done | bytes 2080 | tf_op jit(solution)/shard_map/ppermute | solution.py:34
  15.0 2.7 %collective-permute-start.5 = (f32[2,256]{1,0:T(2,128)S(1)}, f32[2,256]{1,0:T(2,128)S(1)}, u32[]{:S(2)}, u32[]{:S(2)}) collective-permute-start(f32[2,256]{1,0:T(2,128)S(1)} %add.32), channel_id=1, source_target_pairs={{0,17},{1,16},{2,19},{3,18},{4,21},{5,20},{6,23},{7,22},{8,25},{9,... | collective-permute-start | bytes 6152 | tf_op jit(solution)/shard_map/ppermute | solution.py:34
  17.7 1.3 %collective-permute-done.5 = f32[2,256]{1,0:T(2,128)S(1)} collective-permute-done((f32[2,256]{1,0:T(2,128)S(1)}, f32[2,256]{1,0:T(2,128)S(1)}, u32[]{:S(2)}, u32[]{:S(2)}) %collective-permute-start.5) | collective-permute-done | bytes 2080 | tf_op jit(solution)/shard_map/ppermute | solution.py:34
  19.0 0.6 %add_convert_fusion = bf16[2,32,256]{2,1,0:T(8,128)(2,1)} fusion(f32[2,32,256]{2,1,0:T(8,128)S(1)} %get-tuple-element.23, f32[256]{0:T(256)S(1)} %get-tuple-element.26, f32[256]{0:T(256)S(1)} %get-tuple-element.25, f32[256]{0:T(256)S(1)} %add_rsqrt_fusion, f32[256]{0:T(256)S(1)} %bitcast.5), kind=kLoop, calls=%fused_computation | loop fusion | flops 81920 | bytes 102400 | tf_op jit(solution)/shard_map/convert_element_type | solution.py:53
  (6 shorter events, 0.0 us)
Async XLA Ops:
  0.0 1.7 %copy-start = (bf16[2,1024,256]{2,1,0:T(8,128)(2,1)S(1)}, bf16[2,1024,256]{2,1,0:T(8,128)(2,1)}, u32[]{:S(2)}) copy-start(bf16[2,1024,256]{2,1,0:T(8,128)(2,1)} %rows_ref.1) | copy-start | bytes 3145732
  1.1 1.6 %collective-permute-start = (bf16[2,160,256]{2,1,0:T(8,128)(2,1)S(1)}, bf16[2,160,256]{2,1,0:T(8,128)(2,1)S(1)}, u32[]{:S(2)}, u32[]{:S(2)}) collective-permute-start(bf16[2,160,256]{2,1,0:T(8,128)(2,1)S(1)} %get-tuple-element.17.sent_ref), channel_id=1, source_target_pairs={{0,1},{1,0},{2,3},{3,2},{4,5},{5,4},{6,7},{7,6},{8,9},{9,8},{10,11... | collective-permute-start | bytes 491528 | tf_op jit(solution)/shard_map/ppermute | solution.py:275
  3.2 1.5 %collective-permute-start.1 = (f32[2,64,384]{2,1,0:T(8,128)S(1)}, f32[2,64,384]{2,1,0:T(8,128)S(1)}, u32[]{:S(2)}, u32[]{:S(2)}) collective-permute-start(f32[2,64,384]{2,1,0:T(8,128)S(1)} %attend.1.mine_ref), channel_id=1, source_target_pairs={{0,1},{1,0},{2,3},{3,2},{4,5},{5,4},{6,7},{7,6},{8,9},{9,8},{10,11... | collective-permute-start | bytes 589832 | tf_op jit(solution)/shard_map/ppermute | solution.py:312
  4.9 4.0 %collective-permute-start.2 = (f32[2,256]{1,0:T(2,128)S(1)}, f32[2,256]{1,0:T(2,128)S(1)}, u32[]{:S(2)}, u32[]{:S(2)}) collective-permute-start(f32[2,256]{1,0:T(2,128)S(1)} %get-tuple-element.24), channel_id=1, source_target_pairs={{0,3},{1,2},{2,1},{3,0},{4,7},{5,6},{6,5},{7,4},{8,11},{9,10},{10,... | collective-permute-start | bytes 6152 | tf_op jit(solution)/shard_map/ppermute | solution.py:34
  8.9 3.0 %collective-permute-start.3 = (f32[2,256]{1,0:T(2,128)S(1)}, f32[2,256]{1,0:T(2,128)S(1)}, u32[]{:S(2)}, u32[]{:S(2)}) collective-permute-start(f32[2,256]{1,0:T(2,128)S(1)} %add.30), channel_id=1, source_target_pairs={{0,5},{1,4},{2,7},{3,6},{4,1},{5,0},{6,3},{7,2},{8,13},{9,12},{10,... | collective-permute-start | bytes 6152 | tf_op jit(solution)/shard_map/ppermute | solution.py:34
  11.9 3.1 %collective-permute-start.4 = (f32[2,256]{1,0:T(2,128)S(1)}, f32[2,256]{1,0:T(2,128)S(1)}, u32[]{:S(2)}, u32[]{:S(2)}) collective-permute-start(f32[2,256]{1,0:T(2,128)S(1)} %add.31), channel_id=1, source_target_pairs={{0,9},{1,8},{2,11},{3,10},{4,13},{5,12},{6,15},{7,14},{8,1},{9,0},... | collective-permute-start | bytes 6152 | tf_op jit(solution)/shard_map/ppermute | solution.py:34
  15.0 4.0 %collective-permute-start.5 = (f32[2,256]{1,0:T(2,128)S(1)}, f32[2,256]{1,0:T(2,128)S(1)}, u32[]{:S(2)}, u32[]{:S(2)}) collective-permute-start(f32[2,256]{1,0:T(2,128)S(1)} %add.32), channel_id=1, source_target_pairs={{0,17},{1,16},{2,19},{3,18},{4,21},{5,20},{6,23},{7,22},{8,25},{9,... | collective-permute-start | bytes 6152 | tf_op jit(solution)/shard_map/ppermute | solution.py:34

commit v5 on v4

--- a/solution.py
+++ b/solution.py
@@ -112,10 +112,13 @@
     users, group_rows, _ = behaviors_hbm.shape
     tail = group_rows - HALO
     pairs = [
+        *(
+            (behaviors_hbm.at[user, pl.ds(tail, HALO)], sent_ref.at[user, pl.ds(0, HALO)])
+            for user in range(users)
+        ),
+        (mine_hbm, sent_ref.at[:, pl.ds(HALO, mine_hbm.shape[1])]),
         (ranks_hbm, ranks),
         (lengths_hbm, lengths),
-        (mine_hbm, sent_ref.at[:, pl.ds(HALO, mine_hbm.shape[1])]),
-        (behaviors_hbm.at[:, pl.ds(tail, HALO)], sent_ref.at[:, pl.ds(0, HALO)]),
         (planes_hbm, planes_ref),
         (norm_gain_hbm, gain_ref),
         (norm_bias_hbm, bias_ref),
@@ -126,14 +129,14 @@
     ]
     for copy in copies:
         copy.start()
-    for copy in copies[:2]:
+    for copy in copies[users + 1 : users + 3]:
         copy.wait()
     start = lax.axis_index("seq") * group_rows - HALO
     for user in range(users):
         position = ranks[user] + start
         usable = (position >= 0) & (position < lengths[user])
         places_ref[user] = jnp.where(usable, ranks[user], HALO + group_rows)
-    for copy in copies[2:]:
+    for copy in copies[: users + 1] + copies[users + 3 :]:
         copy.wait()
 
 
@@ -266,7 +269,7 @@
         scratch_shapes=[
             pltpu.VMEM(ranks.shape, jnp.int32),
             pltpu.SMEM(lengths.shape, jnp.int32),
-            pltpu.SemaphoreType.DMA((len(arguments),)),
+            pltpu.SemaphoreType.DMA((len(arguments) + users - 1,)),
         ],
         cost_estimate=pl.CostEstimate(flops=LOAD_COST, bytes_accessed=sent_bytes, transcendentals=0),
         compiler_params=params,

time: 19.8 us -> 19.8 us (level)
  no operation moved by 1% of the time
where the time goes in v5:
time: 19.8 us; the launch traced here: 19.6 us
  starting transfers between devices  9.84 us (50%)
  waiting for transfers between devices  6.53 us (33%)
  Pallas kernels  2.54 us (13%)
  other arithmetic  0.66 us (3%)
    ppermute x4, starting transfers between devices, user_total(): value = value + lax.ppermute(value, BOTH, pairs)  8.85 us
    ppermute x4, waiting for transfers between devices, user_total(): value = value + lax.ppermute(value, BOTH, pairs)  5.24 us
    ppermute x1, waiting for transfers between devices, two_groups(): lax.ppermute(part, 'seq', swap)  1.07 us
    pallas_call x1, Pallas kernels, two_groups(): pl.pallas_call(load_kernel, out_shape=(jax.ShapeDtypeStruct((users, HALO...  1.04 us
    pallas_call x1, Pallas kernels, two_groups(): pl.pallas_call(own_picks_kernel, out_shape=(jax.ShapeDtypeStruct((users,...  0.8 us
    convert_element_type x1, other arithmetic, normalized(): return normed.astype(jnp.bfloat16)  0.63 us
    ppermute x1, starting transfers between devices, two_groups(): other = lax.ppermute(sent, 'seq', swap)  0.56 us
    pallas_call x1, Pallas kernels, two_groups(): pl.pallas_call(attend_kernel, out_shape=jax.ShapeDtypeStruct((users, cand...  0.55 us
  transfers between devices with their start and end apart: 6, of which 6 were waited for; matrix products, arithmetic and copies ran while one was open for 0% of the time, Pallas kernels for 4%

profile of v5, /device:TPU:0, one launch (start us, length us, event | category | flops | bytes accessed | tf_op | source)
XLA Modules:
  0.0 19.6 jit_solution(6757749304778943321)
XLA Ops:
  0.0 0.0 copy-start
  0.0 1.0 %load.1 = (bf16[2,160,256]{2,1,0:T(8,128)(2,1)S(1)}, s32[2,1,128]{2,1,0:T(1,128)S(1)}, f32[256]{0:T(256)S(1)}, f32[256]{0:T(256)S(1)}, bf16[64,256]{1,0:T(8,128)(2,1)S(1)}) custom-call(s32[2,1,128]{2,1,0:T(1,128)} %ranks_hbm.1, s32[2]{0:T(128)} %lengths_hbm.1, f32[256]{0:T(256)} %norm_gain_hbm.1, f32[256]{0:T(256)} %norm_bias_hbm.1, ...), custom_call_target="tpu_custom_call" | custom-call | flops 100000000 | bytes 163840 | tf_op jit(solution)/shard_map/load/pallas_call | solution.py:258
  1.0 0.6 %collective-permute-start = (bf16[2,160,256]{2,1,0:T(8,128)(2,1)S(1)}, bf16[2,160,256]{2,1,0:T(8,128)(2,1)S(1)}, u32[]{:S(2)}, u32[]{:S(2)}) collective-permute-start(bf16[2,160,256]{2,1,0:T(8,128)(2,1)S(1)} %get-tuple-element.17.sent_ref), channel_id=1, source_target_pairs={{0,1},{1,0},{2,3},{3,2},{4,5},{5,4},{6,7},{7,6},{8,9},{9,8},{10,11... | collective-permute-start | bytes 491528 | tf_op jit(solution)/shard_map/ppermute | solution.py:278
  1.6 0.0 copy-done
  1.6 0.8 %own_picks.1 = (bf16[2,128,256]{2,1,0:T(8,128)(2,1)S(1)}, bf16[2,128,64]{2,1,0:T(8,128)(2,1)S(1)}, bf16[2,32,64]{2,1,0:T(8,128)(2,1)S(1)}, f32[2,2,128]{2,1,0:T(2,128)S(1)}) custom-call(s32[2,1,128]{2,1,0:T(1,128)S(1)} %get-tuple-element.16.places_ref, bf16[2,1024,256]{2,1,0:T(8,128)(2,1)S(1)} %copy-done, ...), custom_call_target="tpu_custom_call" | custom-call | flops 134217728 | bytes 1048576 | tf_op jit(solution)/shard_map/own_picks/pallas_call | solution.py:279
  2.4 0.2 %collective-permute-done.other_ref = bf16[2,160,256]{2,1,0:T(8,128)(2,1)S(1)} collective-permute-done((bf16[2,160,256]{2,1,0:T(8,128)(2,1)S(1)}, bf16[2,160,256]{2,1,0:T(8,128)(2,1)S(1)}, u32[]{:S(2)}, u32[]{:S(2)}) %collective-permute-start) | collective-permute-done | bytes 163872 | tf_op jit(solution)/shard_map/ppermute | solution.py:278
  2.6 0.6 %attend.1.mine_ref = f32[2,64,384]{2,1,0:T(8,128)S(1)} custom-call(f32[2,2,128]{2,1,0:T(2,128)S(1)} %get-tuple-element.19.masks_ref, bf16[2,128,256]{2,1,0:T(8,128)(2,1)S(1)} %get-tuple-element.20.picked_ref, bf16[2,128,64]{2,1,0:T(8,128)(2,1)S(1)} %get-tuple-element.21.picked_codes_ref, bf16[2,160,256]{2,1,0:T(8,128)(2,1)S(1)} %get-tuple-element.17.sent_ref, ...), custom_call_target="tpu_custom_call" | custom-call | tf_op jit(solution)/shard_map/attend/pallas_call | solution.py:297
  3.2 0.4 %collective-permute-start.1 = (f32[2,64,384]{2,1,0:T(8,128)S(1)}, f32[2,64,384]{2,1,0:T(8,128)S(1)}, u32[]{:S(2)}, u32[]{:S(2)}) collective-permute-start(f32[2,64,384]{2,1,0:T(8,128)S(1)} %attend.1.mine_ref), channel_id=1, source_target_pairs={{0,1},{1,0},{2,3},{3,2},{4,5},{5,4},{6,7},{7,6},{8,9},{9,8},{10,11... | collective-permute-start | bytes 589832 | tf_op jit(solution)/shard_map/ppermute | solution.py:315
  3.6 1.1 %collective-permute-done.1.other_ref = f32[2,64,384]{2,1,0:T(8,128)S(1)} collective-permute-done((f32[2,64,384]{2,1,0:T(8,128)S(1)}, f32[2,64,384]{2,1,0:T(8,128)S(1)}, u32[]{:S(2)}, u32[]{:S(2)}) %collective-permute-start.1) | collective-permute-done | bytes 196640 | tf_op jit(solution)/shard_map/ppermute | solution.py:315
  4.7 0.2 merge.1
  4.9 2.7 %collective-permute-start.2 = (f32[2,256]{1,0:T(2,128)S(1)}, f32[2,256]{1,0:T(2,128)S(1)}, u32[]{:S(2)}, u32[]{:S(2)}) collective-permute-start(f32[2,256]{1,0:T(2,128)S(1)} %get-tuple-element.24), channel_id=1, source_target_pairs={{0,3},{1,2},{2,1},{3,0},{4,7},{5,6},{6,5},{7,4},{8,11},{9,10},{10,... | collective-permute-start | bytes 6152 | tf_op jit(solution)/shard_map/ppermute | solution.py:34
  7.5 1.3 %collective-permute-done.2 = f32[2,256]{1,0:T(2,128)S(1)} collective-permute-done((f32[2,256]{1,0:T(2,128)S(1)}, f32[2,256]{1,0:T(2,128)S(1)}, u32[]{:S(2)}, u32[]{:S(2)}) %collective-permute-start.2) | collective-permute-done | bytes 2080 | tf_op jit(solution)/shard_map/ppermute | solution.py:34
  8.8 1.7 %collective-permute-start.3 = (f32[2,256]{1,0:T(2,128)S(1)}, f32[2,256]{1,0:T(2,128)S(1)}, u32[]{:S(2)}, u32[]{:S(2)}) collective-permute-start(f32[2,256]{1,0:T(2,128)S(1)} %add.30), channel_id=1, source_target_pairs={{0,5},{1,4},{2,7},{3,6},{4,1},{5,0},{6,3},{7,2},{8,13},{9,12},{10,... | collective-permute-start | bytes 6152 | tf_op jit(solution)/shard_map/ppermute | solution.py:34
  10.6 1.3 %collective-permute-done.3 = f32[2,256]{1,0:T(2,128)S(1)} collective-permute-done((f32[2,256]{1,0:T(2,128)S(1)}, f32[2,256]{1,0:T(2,128)S(1)}, u32[]{:S(2)}, u32[]{:S(2)}) %collective-permute-start.3) | collective-permute-done | bytes 2080 | tf_op jit(solution)/shard_map/ppermute | solution.py:34
  11.9 1.8 %collective-permute-start.4 = (f32[2,256]{1,0:T(2,128)S(1)}, f32[2,256]{1,0:T(2,128)S(1)}, u32[]{:S(2)}, u32[]{:S(2)}) collective-permute-start(f32[2,256]{1,0:T(2,128)S(1)} %add.31), channel_id=1, source_target_pairs={{0,9},{1,8},{2,11},{3,10},{4,13},{5,12},{6,15},{7,14},{8,1},{9,0},... | collective-permute-start | bytes 6152 | tf_op jit(solution)/shard_map/ppermute | solution.py:34
  13.6 1.3 %collective-permute-done.4 = f32[2,256]{1,0:T(2,128)S(1)} collective-permute-done((f32[2,256]{1,0:T(2,128)S(1)}, f32[2,256]{1,0:T(2,128)S(1)}, u32[]{:S(2)}, u32[]{:S(2)}) %collective-permute-start.4) | collective-permute-done | bytes 2080 | tf_op jit(solution)/shard_map/ppermute | solution.py:34
  14.9 2.7 %collective-permute-start.5 = (f32[2,256]{1,0:T(2,128)S(1)}, f32[2,256]{1,0:T(2,128)S(1)}, u32[]{:S(2)}, u32[]{:S(2)}) collective-permute-start(f32[2,256]{1,0:T(2,128)S(1)} %add.32), channel_id=1, source_target_pairs={{0,17},{1,16},{2,19},{3,18},{4,21},{5,20},{6,23},{7,22},{8,25},{9,... | collective-permute-start | bytes 6152 | tf_op jit(solution)/shard_map/ppermute | solution.py:34
  17.6 1.3 %collective-permute-done.5 = f32[2,256]{1,0:T(2,128)S(1)} collective-permute-done((f32[2,256]{1,0:T(2,128)S(1)}, f32[2,256]{1,0:T(2,128)S(1)}, u32[]{:S(2)}, u32[]{:S(2)}) %collective-permute-start.5) | collective-permute-done | bytes 2080 | tf_op jit(solution)/shard_map/ppermute | solution.py:34
  19.0 0.6 %add_convert_fusion = bf16[2,32,256]{2,1,0:T(8,128)(2,1)} fusion(f32[2,32,256]{2,1,0:T(8,128)S(1)} %get-tuple-element.23, f32[256]{0:T(256)S(1)} %get-tuple-element.26, f32[256]{0:T(256)S(1)} %get-tuple-element.25, f32[256]{0:T(256)S(1)} %add_rsqrt_fusion, f32[256]{0:T(256)S(1)} %bitcast.5), kind=kLoop, calls=%fused_computation | loop fusion | flops 81920 | bytes 102400 | tf_op jit(solution)/shard_map/convert_element_type | solution.py:53
  (6 shorter events, 0.0 us)
Async XLA Ops:
  0.0 1.6 %copy-start = (bf16[2,1024,256]{2,1,0:T(8,128)(2,1)S(1)}, bf16[2,1024,256]{2,1,0:T(8,128)(2,1)}, u32[]{:S(2)}) copy-start(bf16[2,1024,256]{2,1,0:T(8,128)(2,1)} %rows_ref.1) | copy-start | bytes 3145732
  1.0 1.6 %collective-permute-start = (bf16[2,160,256]{2,1,0:T(8,128)(2,1)S(1)}, bf16[2,160,256]{2,1,0:T(8,128)(2,1)S(1)}, u32[]{:S(2)}, u32[]{:S(2)}) collective-permute-start(bf16[2,160,256]{2,1,0:T(8,128)(2,1)S(1)} %get-tuple-element.17.sent_ref), channel_id=1, source_target_pairs={{0,1},{1,0},{2,3},{3,2},{4,5},{5,4},{6,7},{7,6},{8,9},{9,8},{10,11... | collective-permute-start | bytes 491528 | tf_op jit(solution)/shard_map/ppermute | solution.py:278
  3.2 1.5 %collective-permute-start.1 = (f32[2,64,384]{2,1,0:T(8,128)S(1)}, f32[2,64,384]{2,1,0:T(8,128)S(1)}, u32[]{:S(2)}, u32[]{:S(2)}) collective-permute-start(f32[2,64,384]{2,1,0:T(8,128)S(1)} %attend.1.mine_ref), channel_id=1, source_target_pairs={{0,1},{1,0},{2,3},{3,2},{4,5},{5,4},{6,7},{7,6},{8,9},{9,8},{10,11... | collective-permute-start | bytes 589832 | tf_op jit(solution)/shard_map/ppermute | solution.py:315
  4.9 4.0 %collective-permute-start.2 = (f32[2,256]{1,0:T(2,128)S(1)}, f32[2,256]{1,0:T(2,128)S(1)}, u32[]{:S(2)}, u32[]{:S(2)}) collective-permute-start(f32[2,256]{1,0:T(2,128)S(1)} %get-tuple-element.24), channel_id=1, source_target_pairs={{0,3},{1,2},{2,1},{3,0},{4,7},{5,6},{6,5},{7,4},{8,11},{9,10},{10,... | collective-permute-start | bytes 6152 | tf_op jit(solution)/shard_map/ppermute | solution.py:34
  8.8 3.0 %collective-permute-start.3 = (f32[2,256]{1,0:T(2,128)S(1)}, f32[2,256]{1,0:T(2,128)S(1)}, u32[]{:S(2)}, u32[]{:S(2)}) collective-permute-start(f32[2,256]{1,0:T(2,128)S(1)} %add.30), channel_id=1, source_target_pairs={{0,5},{1,4},{2,7},{3,6},{4,1},{5,0},{6,3},{7,2},{8,13},{9,12},{10,... | collective-permute-start | bytes 6152 | tf_op jit(solution)/shard_map/ppermute | solution.py:34
  11.9 3.1 %collective-permute-start.4 = (f32[2,256]{1,0:T(2,128)S(1)}, f32[2,256]{1,0:T(2,128)S(1)}, u32[]{:S(2)}, u32[]{:S(2)}) collective-permute-start(f32[2,256]{1,0:T(2,128)S(1)} %add.31), channel_id=1, source_target_pairs={{0,9},{1,8},{2,11},{3,10},{4,13},{5,12},{6,15},{7,14},{8,1},{9,0},... | collective-permute-start | bytes 6152 | tf_op jit(solution)/shard_map/ppermute | solution.py:34
  14.9 4.0 %collective-permute-start.5 = (f32[2,256]{1,0:T(2,128)S(1)}, f32[2,256]{1,0:T(2,128)S(1)}, u32[]{:S(2)}, u32[]{:S(2)}) collective-permute-start(f32[2,256]{1,0:T(2,128)S(1)} %add.32), channel_id=1, source_target_pairs={{0,17},{1,16},{2,19},{3,18},{4,21},{5,20},{6,23},{7,22},{8,25},{9,... | collective-permute-start | bytes 6152 | tf_op jit(solution)/shard_map/ppermute | solution.py:34
